TPU v7x, 256 devices: a whole 4x4x8 slice. The times are simulated.
256 devices in a mesh: dp: 256 (over z, y, x, core).
Axes of the slice: x: 4, y: 4, z: 8, core: 2. Of those that a mesh axis runs over, the one named last changes fastest.
Arguments:
- features: bfloat16 [4096, 1024], P('dp')
- w_in: bfloat16 [1024, 1024], replicated
- w_out: bfloat16 [1024, 256], replicated
- item_table: bfloat16 [524288, 256], P('dp')
- cand_ids: int32 [524288], replicated
- log_q: float32 [524288], replicated
- targets: int32 [4096], P('dp')
Outputs:
- output 1: float32 [], replicated
- output 2: float32 [524288, 256], P('dp')
- output 3: float32 [1024, 1024], replicated
- output 4: float32 [1024, 256], replicated
All inputs are finite; a program needn't handle non-finite values.
Results may differ from a plain program's by a relative error of at most 0.001.
Values are sent between devices in bfloat16 or wider.
A program may use at most 768 MiB of HBM per device.

v0:
```python
import jax
import jax.numpy as jnp
from jax import lax
from jax.sharding import PartitionSpec as P


def solution(mesh):
    num_dev = mesh.shape["dp"]

    def local_step(features, w_in, w_out, table_blk, cand_ids, log_q, targets):
        dev_index = lax.axis_index("dp")
        block_rows = table_blk.shape[0]
        cand_dev = cand_ids.shape[0] // num_dev
        tok_total = features.shape[0] * num_dev
        pre_act = jnp.dot(features, w_in, preferred_element_type=jnp.float32)
        act_val, gelu_back = jax.vjp(jax.nn.gelu, pre_act)
        act_b = act_val.astype(jnp.bfloat16)
        query = jnp.dot(act_b, w_out, preferred_element_type=jnp.float32).astype(jnp.bfloat16)
        query_all = lax.all_gather(query, "dp", axis=0, tiled=True)
        tgt_all = lax.all_gather(targets, "dp", axis=0, tiled=True)
        row_base = dev_index * block_rows
        tgt_local = tgt_all - row_base
        tgt_own = (tgt_local >= 0) & (tgt_local < block_rows)
        tgt_index = jnp.clip(tgt_local, 0, block_rows - 1)
        tgt_rows = table_blk[tgt_index]
        own_cands = lax.dynamic_slice_in_dim(cand_ids, dev_index * cand_dev, cand_dev)
        own_logq = lax.dynamic_slice_in_dim(log_q, dev_index * cand_dev, cand_dev)
        cand_index = own_cands - row_base
        cand_rows = table_blk[cand_index]
        tgt_dot = jnp.einsum("td,td->t", query_all, tgt_rows, preferred_element_type=jnp.float32)
        tgt_logit = lax.psum(jnp.where(tgt_own, tgt_dot, 0.0), "dp")
        cand_logit = jnp.einsum("td,cd->tc", query_all, cand_rows, preferred_element_type=jnp.float32) - own_logq[None, :]
        cand_logit = jnp.where(own_cands[None, :] == tgt_all[:, None], -1e9, cand_logit)
        top_val = jnp.maximum(lax.pmax(jnp.max(cand_logit, axis=1), "dp"), tgt_logit)
        exp_sum = lax.psum(jnp.sum(jnp.exp(cand_logit - top_val[:, None]), axis=1), "dp")
        log_norm = top_val + jnp.log(exp_sum + jnp.exp(tgt_logit - top_val))
        loss = jnp.sum(log_norm - tgt_logit) / tok_total
        grad_tgt = (jnp.exp(tgt_logit - log_norm) - 1.0) / tok_total
        cand_grad = (jnp.exp(cand_logit - log_norm[:, None]) / tok_total).astype(jnp.bfloat16)
        own_grad = jnp.where(tgt_own, grad_tgt, 0.0)
        dq_part = own_grad[:, None] * tgt_rows + jnp.einsum("tc,cd->td", cand_grad, cand_rows, preferred_element_type=jnp.float32)
        dq_local = lax.psum_scatter(dq_part, "dp", scatter_dimension=0, tiled=True).astype(jnp.bfloat16)
        grad_cand = jnp.einsum("tc,td->cd", cand_grad, query_all, preferred_element_type=jnp.float32)
        grad_blk = jnp.zeros(table_blk.shape, jnp.float32).at[cand_index].add(grad_cand).at[tgt_index].add(own_grad[:, None] * query_all)
        d_act = jnp.einsum("td,fd->tf", dq_local, w_out, preferred_element_type=jnp.float32)
        d_pre = gelu_back(d_act)[0].astype(jnp.bfloat16)
        grad_w_out = lax.psum(jnp.einsum("tf,td->fd", act_b, dq_local, preferred_element_type=jnp.float32), "dp")
        grad_w_in = lax.psum(jnp.einsum("ti,tf->if", features, d_pre, preferred_element_type=jnp.float32), "dp")
        return loss, grad_blk, grad_w_in, grad_w_out

    return jax.shard_map(local_step, mesh=mesh, in_specs=(P("dp", None), P(), P(), P("dp", None), P(), P(), P("dp")), out_specs=(P(), P("dp", None), P(), P()), check_vma=False)
```

profile of v0, /device:TPU:1, one launch (start us, length us, event | category | flops | bytes accessed | tf_op | source)
XLA Modules:
  0.0 1975.0 jit_solution(2787436839872723021)
XLA Ops:
  7.2 0.0 copy-start
  7.2 0.0 copy-start.2
  7.2 0.0 all-gather.2.cloned.1.call-start
  7.2 1.5 copy-done
  8.8 1.1 fusion.34
  9.9 1.8 convolution_convert_fusion
  11.7 0.0 all-gather.2.cloned.1.call-update
  11.8 0.0 reduce-scatter.2.cloned.1.call-start
  11.8 0.7 dynamic_slice.7
  12.5 0.7 broadcast_clamp_fusion.1
  13.2 0.0 copy-done.2
  13.2 0.0 copy-start.10
  13.2 9.1 gather_fusion
  22.3 0.0 copy-done.10
  22.3 0.2 dynamic-update-slice
  22.5 81.9 %all-reduce = s32[4096]{0:T(1024)S(1)} all-reduce(s32[4096]{0:T(1024)S(1)} %dynamic-update-slice), channel_id=1, replica_groups=mesh['dp'=256] {'dp'}, use_global_device_ids=true, to_apply=%add | all-reduce | flops 4096 | bytes 32768
  104.4 17.0 gather_fusion.1
  121.5 0.0 copy-start.8
  121.5 0.0 all-gather.2.cloned.1.call-done
  121.5 0.0 copy-start.4
  121.5 3.0 fusion.1
  124.5 76.0 %psum.28 = f32[4096]{0:T(1024)S(1)} all-reduce(f32[4096]{0:T(1024)S(1)} %get-tuple-element.16), channel_id=1, replica_groups=mesh['dp'=256] {'dp'}, use_global_device_ids=true, to_apply=%region_2.3 | all-reduce | flops 4096 | bytes 32768 | tf_op jit(solution)/shard_map/psum | solution.py:31
  200.5 0.0 copy-done.8
  200.5 0.0 copy-done.4
  200.5 12.6 fusion
  213.1 72.7 %pmax.7 = f32[4096]{0:T(1024)S(1)} all-reduce(f32[4096]{0:T(1024)S(1)} %get-tuple-element.23), channel_id=1, replica_groups=mesh['dp'=256] {'dp'}, use_global_device_ids=true, to_apply=%region_1.2 | all-reduce | flops 4096 | bytes 32768 | tf_op jit(solution)/shard_map/pmax | solution.py:34
  285.8 15.1 exponential_reduce_fusion
  301.0 73.9 %psum.29 = f32[4096]{0:T(1024)S(1)} all-reduce(f32[4096]{0:T(1024)S(1)} %exponential_reduce_fusion), channel_id=1, replica_groups=mesh['dp'=256] {'dp'}, use_global_device_ids=true, to_apply=%region_4.5 | all-reduce | flops 4096 | bytes 32768 | tf_op jit(solution)/shard_map/psum | solution.py:35
  374.9 0.0 copy-start.5
  374.9 16.0 multiply_convert_fusion
  391.0 0.0 copy-start.3
  391.0 5.7 copy-done.3
  396.7 0.0 copy-done.5
  396.7 6.8 convolution_add_fusion
  403.5 0.0 copy-start.6
  403.5 0.0 copy-start.9
  403.5 0.0 reduce-scatter.2.cloned.1.call-update
  403.5 0.0 all-reduce.4.cloned.1.call-start
  403.6 1277.8 %reduce-scatter.2.cloned.1.call-done = f32[16,256]{1,0:T(8,128)} async-done(((f32[4096,256]{1,0:T(8,128)}), f32[16,256]{1,0:T(8,128)}) %reduce-scatter.2.cloned.1.call-update) | async-done | bytes 16400 | tf_op jit(solution)/shard_map/reduce_scatter | solution.py:42
  1681.4 2.0 fusion.20
  1683.5 0.0 copy-done.6
  1683.5 0.0 copy-done.9
  1683.5 3.7 convolution_bitcast_fusion
  1687.1 0.0 all-reduce.4.cloned.1.call-update
  1687.1 0.6 subtract_reduce_fusion
  1688.4 9.5 fusion.35
  1697.9 13.4 scatter_custom_fusion
  1711.2 33.4 %scatter_custom_fusion.1 = f32[2048,256]{1,0:T(8,128)} fusion(f32[2048,256]{1,0:T(8,128)} %scatter_custom_fusion, s32[4096]{0:T(1024)S(1)} %get-tuple-element.19, bf16[4096,256]{1,0:T(8,128)(2,1)S(1)} %copy-done.4, f32[4096]{0:T(1024)S(1)} %get-tuple-element.14), kind=kCustom, calls=%fused_computation.13 | custom fusion | flops 3145728 | bytes 4210688 | tf_op jit(solution)/shard_map/scatter-add | solution.py:44
  1744.6 216.2 %all-reduce.4.cloned.1.call-done = (f32[1024,1024]{0,1:T(8,128)}, f32[1024,256]{1,0:T(8,128)}) async-done(((f32[1024,1024]{0,1:T(8,128)}, f32[1024,256]{1,0:T(8,128)}), (f32[1024,1024]{0,1:T(8,128)}, f32[1024,256]{1,0:T(8,128)})) %all-reduce.4.cloned.1.call-update) | async-done | bytes 5242896 | tf_op jit(solution)/shard_map/psum | solution.py:48
  1960.8 0.0 copy-start.1
  1960.8 0.0 copy-start.7
  1960.8 5.5 copy.12
  1966.3 0.0 copy-done.7
  1966.3 1.0 copy.22
  1967.3 0.0 copy-done.1
  (5 shorter events, 0.0 us)
Async XLA Ops:
  7.2 1.6 copy-start
  7.2 6.0 copy-start.2
  7.2 114.3 %all-gather.2.cloned.1.call-start = ((), (), s32[]{:S(2)}) async-start(), calls=%async_computation.1 | async-start | bytes 2105344 | tf_op jit(solution)/shard_map/all_gather | solution.py:19
  11.8 1669.7 %reduce-scatter.2.cloned.1.call-start = ((), (), s32[]{:S(2)}) async-start(), calls=%async_computation.2 | async-start | bytes 4210688 | tf_op jit(solution)/shard_map/reduce_scatter | solution.py:42
  13.2 9.1 copy-start.10
  121.5 79.0 %copy-start.8 = (bf16[2048,256]{1,0:T(8,128)(2,1)S(1)}, bf16[2048,256]{1,0:T(8,128)(2,1)}, u32[]{:S(2)}) copy-start(bf16[2048,256]{1,0:T(8,128)(2,1)} %gather_fusion) | copy-start | bytes 3145732
  121.5 79.0 %copy-start.4 = (bf16[4096,256]{1,0:T(8,128)(2,1)S(1)}, bf16[4096,256]{1,0:T(8,128)(2,1)}, u32[]{:S(2)}) copy-start(bf16[4096,256]{1,0:T(8,128)(2,1)} %all-gather.2.cloned.1.call-done) | copy-start | bytes 6291460
  374.9 21.8 %copy-start.5 = (bf16[4096,256]{1,0:T(8,128)(2,1)S(1)}, bf16[4096,256]{1,0:T(8,128)(2,1)}, u32[]{:S(2)}) copy-start(bf16[4096,256]{1,0:T(8,128)(2,1)} %gather_fusion.1) | copy-start | bytes 6291460
  391.0 5.7 copy-start.3
  403.5 1280.0 %copy-start.6 = (bf16[1024,256]{1,0:T(8,128)(2,1)S(1)}, bf16[1024,256]{1,0:T(8,128)(2,1)}, u32[]{:S(2)}) copy-start(bf16[1024,256]{1,0:T(8,128)(2,1)} %param.9) | copy-start | bytes 1572868
  403.5 1280.0 %copy-start.9 = (bf16[16,1024]{1,0:T(8,128)(2,1)S(1)}, bf16[16,1024]{1,0:T(8,128)(2,1)}, u32[]{:S(2)}) copy-start(bf16[16,1024]{1,0:T(8,128)(2,1)} %param.7) | copy-start | bytes 98308
  403.5 1557.3 %all-reduce.4.cloned.1.call-start = ((), (), s32[]{:S(2)}) async-start(), calls=%async_computation.3 | async-start | bytes 10485760 | tf_op jit(solution)/shard_map/psum | solution.py:48
  1960.8 6.5 copy-start.1
  1960.8 5.5 copy-start.7
Sparse Core Ops, SparseCore 0:
  12.3 108.2 all-gather.1
  403.6 1277.7 reduce-scatter.1
  1687.6 273.2 all-reduce.3
where the time goes:
time: 1980 us; the launch traced here: 1970 us
  waiting for transfers between devices  1490 us (75%)
  blocking collectives  304 us (15%)
  other arithmetic  82.3 us (4%)
  local copies, waits for them, and re-layouts  40.8 us (2%)
  matrix products  37.6 us (2%)
    reduce_scatter x1, waiting for transfers between devices, local_step(): lax.psum_scatter(dq_part, 'dp', scatter_dimension=0, tiled=True)  1280 us
    psum x1, waiting for transfers between devices, local_step(): lax.psum(jnp.einsum('ti,tf->if', features, d_pre, preferred_element_type=...  216 us
    unnamed x1, blocking collectives  81.9 us
    psum x1, blocking collectives, local_step(): tgt_logit = lax.psum(jnp.where(tgt_own, tgt_dot, 0.0), 'dp')  76 us
    psum x1, blocking collectives, local_step(): lax.psum(jnp.sum(jnp.exp(cand_logit - top_val[:, None]), axis=1), 'dp')  73.9 us
    pmax x1, blocking collectives, local_step(): lax.pmax(jnp.max(cand_logit, axis=1), 'dp')  72.7 us
    scatter-add x2, other arithmetic, local_step(): jnp.zeros(table_blk.shape, jnp.float32).at[cand_index].add(grad_cand)  46.7 us
  transfers between devices with their start and end apart: 3, of which 2 were waited for; matrix products, arithmetic and copies ran while one was open for 4% of the time, Pallas kernels for 0%

commit v1 on v0

v1 whole, which is shorter than its diff:
```python
import functools
import jax
import jax.numpy as jnp
from jax import lax
from jax.experimental import pallas as pl
from jax.experimental.pallas import tpu as pltpu
from jax.sharding import PartitionSpec as P

NZ, NY, NX = 8, 4, 4
LANES = 128
CHIP_TOK = 32
DEV_TOK = 16
MIB = 1 << 20
MESH = pl.DeviceIdType.MESH


def coords():
    me = lax.axis_index("dp")
    return me // (NY * NX * 2), (me // (NX * 2)) % NY, (me // 2) % NX, me % 2


def dev(z, y, x, c):
    return (((z * NY + y) * NX + x) * 2 + c,)


def rcopy(src, dst, ssem, rsem, to):
    return pltpu.make_async_remote_copy(src_ref=src, dst_ref=dst, send_sem=ssem, recv_sem=rsem, device_id=to, device_id_type=MESH)


def entry_barrier(z, y, x, c):
    bar = pltpu.get_barrier_semaphore()
    peers = [dev(z, y, x, 1 - c)]
    peers += [dev(z, y, (x + k) % NX, c) for k in range(1, NX)]
    peers += [dev(z, (y + k) % NY, x, c) for k in range(1, NY)]
    peers += [dev((z + k) % NZ, y, x, c) for k in range(1, NZ)]
    for p in peers:
        pl.semaphore_signal(bar, inc=1, device_id=p, device_id_type=MESH)
    pl.semaphore_wait(bar, len(peers))


def ag_tail(out_ref, z, y, x, c, s1, r1, s2, r2, s3, r3, sd, rd):
    blk = out_ref.at[c, z, y, x]
    to_c = dev(z, y, x, 1 - c)
    c1 = [rcopy(blk, blk, s1.at[k - 1], r1.at[k - 1], dev((z + k) % NZ, y, x, c)) for k in range(1, NZ)]
    for cp in c1:
        cp.start()
    for cp in c1:
        cp.wait()
    col = out_ref.at[c, :, y, x]
    c2 = [rcopy(col, col, s2.at[k - 1], r2.at[k - 1], dev(z, (y + k * (1 - c)) % NY, (x + k * c) % NX, c)) for k in range(1, 4)]
    for cp in c2:
        cp.start()
    dc = [rcopy(col, col, sd.at[0], rd.at[0], to_c)]
    dc[0].start()
    for cp in c2:
        cp.wait()

    def last(sl, to, got):
        c3 = [rcopy(sl, sl, s3.at[k - 1], r3.at[k - 1], to(k)) for k in range(1, 4)]
        for cp in c3:
            cp.start()
        dd = []
        for k in range(1, 4):
            g = got(k, 2)
            dd.append(rcopy(g, g, sd.at[k], rd.at[k], to_c))
            dd[-1].start()
        for k in (1, 3, 2):
            c3[k - 1].wait()
            g = got(k, 3)
            dd.append(rcopy(g, g, sd.at[3 + k], rd.at[3 + k], to_c))
            dd[-1].start()
        for cp in dd:
            cp.wait_send()

    @pl.when(c == 0)
    def _():
        last(out_ref.at[0, :, :, x], lambda k: dev(z, y, (x + k) % NX, c),
             lambda k, ph: out_ref.at[0, :, (y + NY - k) % NY, x] if ph == 2 else out_ref.at[0, :, :, (x + NX - k) % NX])

    @pl.when(c == 1)
    def _():
        last(out_ref.at[1, :, y, :], lambda k: dev(z, (y + k) % NY, x, c),
             lambda k, ph: out_ref.at[1, :, y, (x + NX - k) % NX] if ph == 2 else out_ref.at[1, :, (y + NY - k) % NY, :])

    dc[0].wait()
    for k in range(1, 4):
        rcopy(col, col, sd.at[k], rd.at[k], to_c).wait_recv()
        pln = out_ref.at[0, :, :, 0]
        rcopy(pln, pln, sd.at[3 + k], rd.at[3 + k], to_c).wait_recv()


def ag_start(src_ref, out_ref, z, y, x, c, loc_sem, ssem, rsem):
    half = out_ref.shape[-1]
    mine = pl.ds(pl.multiple_of(c * half, half), half)
    other = pl.ds(pl.multiple_of((1 - c) * half, half), half)
    rows = pl.ds(pl.multiple_of(c * DEV_TOK, DEV_TOK), DEV_TOK)
    cp0 = rcopy(src_ref.at[:, other], out_ref.at[1 - c, z, y, x, rows, :], ssem, rsem, dev(z, y, x, 1 - c))
    cp0.start()
    cl = pltpu.make_async_copy(src_ref.at[:, mine], out_ref.at[c, z, y, x, rows, :], loc_sem)
    cl.start()
    cl.wait()
    cp0.wait()


def ag_kernel(src_ref, out_ref, loc_sem, ssem, rsem, *sems):
    z, y, x, c = coords()
    entry_barrier(z, y, x, c)
    ag_start(src_ref, out_ref, z, y, x, c, loc_sem, ssem, rsem)
    ag_tail(out_ref, z, y, x, c, *sems)


def ag_y_kernel(src_ref, y_ref, out_ref, yout_ref, ytmp, loc_sem, ssem, rsem, t1, q1, t2, q2, t3, q3, t4, q4, *sems):
    z, y, x, c = coords()
    entry_barrier(z, y, x, c)
    cy = rcopy(y_ref, ytmp, t1, q1, dev(z, y, x, 1 - c))
    cy.start()
    ag_start(src_ref, out_ref, z, y, x, c, loc_sem, ssem, rsem)
    cy.wait()
    yout_ref[z, y, x] = y_ref[...] + ytmp[...]
    for axis, to, sl, ts, qs in (
        (NX, lambda k: dev(z, y, (x + k) % NX, c), yout_ref.at[z, y, x], t2, q2),
        (NY, lambda k: dev(z, (y + k) % NY, x, c), yout_ref.at[z, y], t3, q3),
        (NZ, lambda k: dev((z + k) % NZ, y, x, c), yout_ref.at[z], t4, q4),
    ):
        cps = [rcopy(sl, sl, ts.at[k - 1], qs.at[k - 1], to(k)) for k in range(1, axis)]
        for cp in cps:
            cp.start()
        for cp in cps:
            cp.wait()
    ag_tail(out_ref, z, y, x, c, *sems)


_D = pltpu.SemaphoreType.DMA
_AG_SEMS = [_D((7,)), _D((7,)), _D((3,)), _D((3,)), _D((3,)), _D((3,)), _D((7,)), _D((7,))]


def all_gather(src, cid, name):
    cols = src.shape[1]
    return pl.pallas_call(
        ag_kernel, name=name,
        out_shape=jax.ShapeDtypeStruct((2, NZ, NY, NX, CHIP_TOK, cols // 2), src.dtype),
        in_specs=[pl.BlockSpec(memory_space=pl.ANY)],
        out_specs=pl.BlockSpec(memory_space=pltpu.VMEM),
        scratch_shapes=[_D, _D, _D] + _AG_SEMS,
        compiler_params=pltpu.CompilerParams(collective_id=cid, has_side_effects=True, vmem_limit_bytes=40 * MIB),
    )(src)


def all_gather_y(src, yrow, cid, name):
    cols = src.shape[1]
    V = pl.BlockSpec(memory_space=pltpu.VMEM)
    return pl.pallas_call(
        ag_y_kernel, name=name,
        out_shape=(jax.ShapeDtypeStruct((2, NZ, NY, NX, CHIP_TOK, cols // 2), src.dtype), jax.ShapeDtypeStruct((NZ, NY, NX, 1, LANES), jnp.int32)),
        in_specs=[pl.BlockSpec(memory_space=pl.ANY), V],
        out_specs=(V, V),
        scratch_shapes=[pltpu.VMEM((1, LANES), jnp.int32), _D, _D, _D, _D, _D, _D((3,)), _D((3,)), _D((3,)), _D((3,)), _D((7,)), _D((7,))] + _AG_SEMS,
        compiler_params=pltpu.CompilerParams(collective_id=cid, has_side_effects=True, vmem_limit_bytes=40 * MIB),
    )(src, yrow)


def ag_rows(full):
    return jnp.concatenate([full[0].reshape(-1, full.shape[-1]), full[1].reshape(-1, full.shape[-1])], axis=1)


NEG = -jnp.inf
CH = NY * NX * CHIP_TOK


def lane_row_to_col(row):
    return jnp.transpose(jnp.broadcast_to(row, (LANES, LANES)))


def logq_rows(cid_v, lq_v, lqr_ref, base):
    for blk in range(lqr_ref.shape[1] // LANES):
        rid = lax.broadcasted_iota(jnp.int32, (LANES, LANES), 0) + (base + blk * LANES)
        acc = jnp.zeros((LANES, LANES), jnp.float32)
        for q in range(DEV_TOK):
            acc += jnp.where(cid_v[q:q + 1, :] == rid, lq_v[q:q + 1, :], 0.0)
        col = jnp.broadcast_to(jnp.sum(acc, axis=1, keepdims=True), (LANES, LANES))
        lqr_ref[:, blk * LANES:(blk + 1) * LANES] = jnp.transpose(col)[:8]


def scores_chunk(h, emb_ref, lqr_ref, e_ref, d_ref, mcol_ref, zcol_ref, scol_ref):
    rows = emb_ref.shape[0]
    RB = 64
    for j in range(0, rows, 256):
        s = lax.dot_general(h, emb_ref[j:j + 256, :], (((1,), (1,)), ((), ())), preferred_element_type=jnp.float32)
        for rb in range(0, CH, RB):
            rs = slice(rb, rb + RB)
            m = mcol_ref[rs, :] if j else jnp.full((RB, LANES), NEG, jnp.float32)
            zc = zcol_ref[rs, :] if j else jnp.full((RB, LANES), NEG, jnp.float32)
            d = d_ref[rs, :]
            for k in (0, LANES):
                raw = s[rs, k:k + LANES]
                hit = d == float(j + k)
                zc = jnp.where(hit, raw, zc)
                v = jnp.where(hit, -1e9, raw - lqr_ref[:1, j + k:j + k + LANES])
                e_ref[rs, j + k:j + k + LANES] = v
                m = jnp.maximum(m, v)
            mcol_ref[rs, :] = m
            zcol_ref[rs, :] = zc
    for rb in range(0, CH, RB):
        rs = slice(rb, rb + RB)
        zc = jnp.max(zcol_ref[rs, :], axis=1, keepdims=True)
        m = jnp.maximum(jnp.max(mcol_ref[rs, :], axis=1, keepdims=True), zc)
        zcol_ref[rs, :] = jnp.broadcast_to(zc, (RB, LANES))
        mcol_ref[rs, :] = jnp.broadcast_to(m, (RB, LANES))

    def grp(g, _):
        rs = pl.ds(pl.multiple_of(g * CHIP_TOK, CHIP_TOK), CHIP_TOK)
        m = mcol_ref[rs, :]
        tot = jnp.zeros((CHIP_TOK, LANES), jnp.float32)
        for k in range(0, rows, LANES):
            ex = jnp.exp(e_ref[rs, k:k + LANES] - m)
            e_ref[rs, k:k + LANES] = ex
            tot += ex
        scol_ref[rs, :] = tot
        return 0
    lax.fori_loop(0, CH // CHIP_TOK, grp, 0)
    for rb in range(0, CH, RB):
        rs = slice(rb, rb + RB)
        tot = jnp.sum(scol_ref[rs, :], axis=1, keepdims=True)
        scol_ref[rs, :] = jnp.broadcast_to(tot, (RB, LANES)) + jnp.exp(zcol_ref[rs, :] - mcol_ref[rs, :])


def scores_kernel(h_ref, emb_ref, y_ref, cid_hbm, lq_hbm, e_ref, mcol_ref, mrow_ref, srow_ref, zrow_ref,
                  cid_v, lq_v, lqr_ref, d_ref, zcol_ref, scol_ref, sem):
    zi = pl.program_id(0)
    me = lax.axis_index("dp")
    rows = emb_ref.shape[0]
    base = me * rows

    @pl.when(zi == 0)
    def _():
        own = pl.ds(me * DEV_TOK, DEV_TOK)
        ca = pltpu.make_async_copy(cid_hbm.at[own], cid_v, sem.at[0])
        cb = pltpu.make_async_copy(lq_hbm.at[own], lq_v, sem.at[1])
        ca.start()
        cb.start()
        ca.wait()
        cb.wait()
        logq_rows(cid_v, lq_v, lqr_ref, base)

    lane = lax.broadcasted_iota(jnp.int32, (LANES, LANES), 1).astype(jnp.float32)
    for b in range(CH // LANES):
        yr = jnp.sum(y_ref[0, b, :, 0, :], axis=0, keepdims=True) - base
        d_ref[b * LANES:(b + 1) * LANES, :] = lane_row_to_col(yr.astype(jnp.float32)) - lane
    h = jnp.concatenate([h_ref[0, 0].reshape(CH, LANES), h_ref[1, 0].reshape(CH, LANES)], axis=1)
    scores_chunk(h, emb_ref, lqr_ref, e_ref, d_ref, mcol_ref, zcol_ref, scol_ref)
    for b in range(CH // LANES):
        bs = slice(b * LANES, (b + 1) * LANES)
        row = pl.ds(zi * (CH // LANES) + b, 1)
        mrow_ref[row, :] = jnp.transpose(mcol_ref[bs, :])[:1]
        srow_ref[row, :] = jnp.transpose(scol_ref[bs, :])[:1]
        zrow_ref[row, :] = jnp.transpose(zcol_ref[bs, :])[:1]


def scores(hfull, emb, yfull, cand_ids, log_q):
    rows = emb.shape[0]
    tok = NZ * CH
    whole = lambda *s: pl.BlockSpec(s, lambda i: (0,) * len(s))
    return pl.pallas_call(
        scores_kernel, name="scores", grid=(NZ,),
        out_shape=(jax.ShapeDtypeStruct((tok, rows), jnp.float32),
                   jax.ShapeDtypeStruct((tok, LANES), jnp.float32), jax.ShapeDtypeStruct((tok // LANES, LANES), jnp.float32),
                   jax.ShapeDtypeStruct((tok // LANES, LANES), jnp.float32), jax.ShapeDtypeStruct((tok // LANES, LANES), jnp.float32)),
        in_specs=[pl.BlockSpec((2, 1, NY, NX, CHIP_TOK, LANES), lambda i: (0, i, 0, 0, 0, 0)), whole(rows, 256),
                  pl.BlockSpec((1, NY, NX, 1, LANES), lambda i: (i, 0, 0, 0, 0)), pl.BlockSpec(memory_space=pl.ANY), pl.BlockSpec(memory_space=pl.ANY)],
        out_specs=(pl.BlockSpec((CH, rows), lambda i: (i, 0)),
                   pl.BlockSpec((CH, LANES), lambda i: (i, 0)), whole(tok // LANES, LANES), whole(tok // LANES, LANES), whole(tok // LANES, LANES)),
        scratch_shapes=[pltpu.VMEM((DEV_TOK, LANES), jnp.int32), pltpu.VMEM((DEV_TOK, LANES), jnp.float32), pltpu.VMEM((8, rows), jnp.float32),
                        pltpu.VMEM((CH, LANES), jnp.float32), pltpu.VMEM((CH, LANES), jnp.float32), pltpu.VMEM((CH, LANES), jnp.float32),
                        pltpu.SemaphoreType.DMA((2,))],
        compiler_params=pltpu.CompilerParams(vmem_limit_bytes=48 * MIB),
    )(hfull, emb, yfull, cand_ids.reshape(-1, LANES), log_q.reshape(-1, LANES))


HR = DEV_TOK


def merge_stats(parts):
    m = functools.reduce(jnp.maximum, [p[:HR] for p in parts])
    s = sum(p[HR:2 * HR] * jnp.exp(p[:HR] - m) for p in parts)
    t = sum(p[2 * HR:] for p in parts)
    return m, s, t


def put_stats(ref, parts):
    m, s, t = merge_stats(parts)
    ref[0:HR, :] = m
    ref[HR:2 * HR, :] = s
    ref[2 * HR:, :] = t


def stats_kernel(m_ref, s_ref, z_ref, l_ref, loss_ref, b0, bc, bx, by, bz, fin, sc, rc, sx, rx, sy, ry, sz, rz, sf, rf):
    z, y, x, c = coords()
    entry_barrier(z, y, x, c)
    for hf in range(2):
        hs = slice(hf * HR, (hf + 1) * HR)
        zz = z_ref[hs, :]
        zz = jnp.where(zz > NEG, zz, 0.0)
        b0[hf, 0:HR, :] = m_ref[hs, :]
        b0[hf, HR:2 * HR, :] = s_ref[hs, :]
        b0[hf, 2 * HR:, :] = zz[:8] + zz[8:]
    cp = rcopy(b0.at[1 - c], bc, sc, rc, dev(z, y, x, 1 - c))
    cp.start()
    cp.wait()
    here, there = b0[c], bc[...]
    even = c == 0
    put_stats(bx.at[x], [jnp.where(even, here, there), jnp.where(even, there, here)])
    cps = [rcopy(bx.at[x], bx.at[x], sx.at[k - 1], rx.at[k - 1], dev(z, y, (x + k) % NX, c)) for k in range(1, NX)]
    [cp.start() for cp in cps]
    [cp.wait() for cp in cps]
    put_stats(by.at[y], [bx[i] for i in range(NX)])
    cps = [rcopy(by.at[y], by.at[y], sy.at[k - 1], ry.at[k - 1], dev(z, (y + k) % NY, x, c)) for k in range(1, NY)]
    [cp.start() for cp in cps]
    [cp.wait() for cp in cps]
    put_stats(bz.at[z], [by[i] for i in range(NY)])
    cps = [rcopy(bz.at[z], bz.at[z], sz.at[k - 1], rz.at[k - 1], dev((z + k) % NZ, y, x, c)) for k in range(1, NZ)]
    [cp.start() for cp in cps]
    [cp.wait() for cp in cps]
    m, s, t = merge_stats([bz[i] for i in range(NZ)])
    fin[c, 0:HR, :] = m + jnp.log(s)
    fin[c, HR:, :] = t
    cp = rcopy(fin.at[c], fin.at[c], sf, rf, dev(z, y, x, 1 - c))
    cp.start()
    cp.wait()
    ls = fin[0, 0:HR, :] + fin[1, 0:HR, :]
    ls = ls[:8] + ls[8:] - (fin[0, HR:, :] + fin[1, HR:, :])
    l_ref[0:HR, :] = fin[0, 0:HR, :]
    l_ref[HR:, :] = fin[1, 0:HR, :]
    tot = jnp.sum(jnp.sum(ls, axis=0, keepdims=True), axis=1, keepdims=True)
    loss_ref[...] = jnp.broadcast_to(tot * (1.0 / (NZ * CH)), (8, LANES))


def stats(mrow, srow, zrow, cid):
    V = pl.BlockSpec(memory_space=pltpu.VMEM)
    D = pltpu.SemaphoreType.DMA
    buf = lambda n: pltpu.VMEM((n, 40, LANES), jnp.float32)
    return pl.pallas_call(
        stats_kernel, name="stats",
        out_shape=(jax.ShapeDtypeStruct(mrow.shape, jnp.float32), jax.ShapeDtypeStruct((8, LANES), jnp.float32)),
        in_specs=[V] * 3, out_specs=(V, V),
        scratch_shapes=[buf(2), pltpu.VMEM((40, LANES), jnp.float32), buf(NX), buf(NY), buf(NZ), pltpu.VMEM((2, 24, LANES), jnp.float32),
                        D, D, D((3,)), D((3,)), D((3,)), D((3,)), D((7,)), D((7,)), D, D],
        compiler_params=pltpu.CompilerParams(collective_id=cid, has_side_effects=True),
    )(mrow, srow, zrow)


def grad_kernel(e_hbm, mcol_hbm, h_ref, emb_ref, y_ref, l_ref, z_ref, dh_ref, de_ref,
                ebuf, mbuf, p_ref, d_ref, dq, rc, a0, ra, a1, rb, zb, esem, msem,
                sc, rcs, sa, ras, sb, rbs, sz, rzs, s1, r1, s2, r2, s3, r3, sd, rd):
    z, y, x, c = coords()
    me = lax.axis_index("dp")
    rows = emb_ref.shape[0]
    base = me * rows
    ax1 = x * (1 - c) + y * c
    ax2 = y * (1 - c) + x * c
    to_c = dev(z, y, x, 1 - c)
    to_1 = lambda k: dev(z, (y + k * c) % NY, (x + k * (1 - c)) % NX, c)
    to_2 = lambda k: dev(z, (y + k * (1 - c)) % NY, (x + k * c) % NX, c)

    def chunk(k):
        return (z + 1 + k) % NZ

    def load(k, slot):
        ch = chunk(k)
        return (pltpu.make_async_copy(e_hbm.at[pl.ds(pl.multiple_of(ch * CH, CH), CH)], ebuf.at[slot], esem.at[slot]),
                pltpu.make_async_copy(mcol_hbm.at[pl.ds(pl.multiple_of(ch * CH, CH), CH)], mbuf.at[slot], msem.at[slot]))

    for cp in load(0, 0):
        cp.start()
    entry_barrier(z, y, x, c)
    de_ref[...] = jnp.zeros_like(de_ref)
    lane = lax.broadcasted_iota(jnp.int32, (LANES, LANES), 1).astype(jnp.float32)
    c_copy = lambda k: rcopy(dq.at[k, 1 - c], rc.at[k], sc.at[k], rcs.at[k], to_c)
    a_copy = lambda k, j: rcopy(a0.at[k, (ax1 + j) % 4], ra.at[k, ax1], sa.at[k, j - 1], ras.at[k, j - 1], to_1(j))
    b_copy = lambda k, j: rcopy(a1.at[k, (ax2 + j) % 4], rb.at[k, ax2], sb.at[k, j - 1], rbs.at[k, j - 1], to_2(j))
    z_copy = lambda k: rcopy(zb.at[NZ + k], zb.at[z], sz.at[k], rzs.at[k], dev(chunk(k), y, x, c))

    def body(k, _):
        @pl.when(k < NZ)
        def _():
            slot = lax.rem(k, 2)
            ch = chunk(k)

            @pl.when(k + 1 < NZ)
            def _():
                for cp in load(k + 1, 1 - slot):
                    cp.start()
            for cp in load(k, slot):
                cp.wait()
            for b in range(CH // LANES):
                bs = slice(b * LANES, (b + 1) * LANES)
                row = pl.ds(ch * (CH // LANES) + b, 1)
                lcol = lane_row_to_col(l_ref[row, :])
                sc_col = jnp.exp(mbuf[slot, bs, :] - lcol) * (1.0 / (NZ * CH))
                yr = jnp.sum(y_ref[ch, b, :, 0, :], axis=0, keepdims=True) - base
                d_ref[bs, :] = lane_row_to_col(yr.astype(jnp.float32)) - lane
                for q in range(0, rows, LANES):
                    p_ref[bs, q:q + LANES] = (ebuf[slot, bs, q:q + LANES] * sc_col).astype(jnp.bfloat16)
            h = jnp.concatenate([h_ref[0, ch].reshape(CH, LANES), h_ref[1, ch].reshape(CH, LANES)], axis=1)
            for q in range(0, rows, 512):
                de_ref[q:q + 512, :] += lax.dot_general(p_ref[:, q:q + 512], h, (((0,), (0,)), ((), ())), preferred_element_type=jnp.float32)
            dqv = jnp.dot(p_ref[...], emb_ref[...], preferred_element_type=jnp.float32)
            for q in range(0, rows, LANES):
                p_ref[:, q:q + LANES] = jnp.where(d_ref[...] == float(q), 1.0, 0.0).astype(jnp.bfloat16)
            tgt = jnp.dot(p_ref[...], emb_ref[...], preferred_element_type=jnp.float32)
            for b in range(CH // LANES):
                bs = slice(b * LANES, (b + 1) * LANES)
                row = pl.ds(ch * (CH // LANES) + b, 1)
                zr = z_ref[row, :]
                g = jnp.where(zr > NEG, (jnp.exp(zr - l_ref[row, :]) - 1.0) * (1.0 / (NZ * CH)), 0.0)
                gc = lane_row_to_col(g)
                for hf in range(2):
                    v = dqv[bs, hf * LANES:hf * LANES + LANES] + gc * tgt[bs, hf * LANES:hf * LANES + LANES]
                    dq[k, hf, b] = v.reshape(NX, CHIP_TOK, LANES)
            c_copy(k).start()

        @pl.when((k >= 1) & (k <= NZ))
        def _():
            q = k - 1
            c_copy(q).wait()
            for yy in range(NY):
                for xx in range(NX):
                    i1 = xx * (1 - c) + yy * c
                    i2 = yy * (1 - c) + xx * c
                    a0[q, i1, i2] = dq[q, c, yy, xx] + rc[q, yy, xx]
            for j in range(1, 4):
                a_copy(q, j).start()

        @pl.when((k >= 2) & (k <= NZ + 1))
        def _():
            q = k - 2
            for j in range(1, 4):
                a_copy(q, j).wait()
            ra[q, ax1] = a0[q, ax1]
            a1[q] = (ra[q, 0] + ra[q, 1]) + (ra[q, 2] + ra[q, 3])
            for j in range(1, 4):
                b_copy(q, j).start()

        @pl.when((k >= 3) & (k <= NZ + 2))
        def _():
            q = k - 3
            for j in range(1, 4):
                b_copy(q, j).wait()
            rb[q, ax2] = a1[q, ax2]
            v = (rb[q, 0] + rb[q, 1]) + (rb[q, 2] + rb[q, 3])

            @pl.when(q < NZ - 1)
            def _():
                zb[NZ + q] = v
                z_copy(q).start()

            @pl.when(q == NZ - 1)
            def _():
                zb[z] = v
        return 0

    lax.fori_loop(0, NZ + 3, body, 0)
    for k in range(NZ - 1):
        z_copy(k).wait()
    tot = ((zb[0] + zb[1]) + (zb[2] + zb[3])) + ((zb[4] + zb[5]) + (zb[6] + zb[7]))
    dh_ref[c, z, y, x] = tot.astype(jnp.bfloat16)
    ag_tail(dh_ref, z, y, x, c, s1, r1, s2, r2, s3, r3, sd, rd)


def grads(e, mcol, hfull, emb, yfull, lrow, zrow, cid):
    V = pl.BlockSpec(memory_space=pltpu.VMEM)
    A = pl.BlockSpec(memory_space=pl.ANY)
    D = pltpu.SemaphoreType.DMA
    F = jnp.float32
    rows = emb.shape[0]
    return pl.pallas_call(
        grad_kernel, name="grads",
        out_shape=(jax.ShapeDtypeStruct((2, NZ, NY, NX, CHIP_TOK, LANES), jnp.bfloat16), jax.ShapeDtypeStruct((rows, 256), F)),
        in_specs=[A, A, V, V, V, V, V], out_specs=(V, V),
        scratch_shapes=[pltpu.VMEM((2, CH, rows), F), pltpu.VMEM((2, CH, LANES), F), pltpu.VMEM((CH, rows), jnp.bfloat16), pltpu.VMEM((CH, LANES), F),
                        pltpu.VMEM((NZ, 2, NY, NX, CHIP_TOK, LANES), F), pltpu.VMEM((NZ, NY, NX, CHIP_TOK, LANES), F),
                        pltpu.VMEM((NZ, 4, 4, CHIP_TOK, LANES), F), pltpu.VMEM((NZ, 4, 4, CHIP_TOK, LANES), F),
                        pltpu.VMEM((NZ, 4, CHIP_TOK, LANES), F), pltpu.VMEM((NZ, 4, CHIP_TOK, LANES), F), pltpu.VMEM((2 * NZ, CHIP_TOK, LANES), F),
                        D((2,)), D((2,)), D((NZ,)), D((NZ,)), D((NZ, 3)), D((NZ, 3)), D((NZ, 3)), D((NZ, 3)), D((NZ - 1,)), D((NZ - 1,)),
                        D((7,)), D((7,)), D((3,)), D((3,)), D((3,)), D((3,)), D((7,)), D((7,))],
        compiler_params=pltpu.CompilerParams(collective_id=cid, has_side_effects=True, vmem_limit_bytes=60 * MIB),
    )(e, mcol, hfull, emb, yfull, lrow, zrow)


def fix_kernel(de_ref, h_ref, y_ref, l_ref, z_ref, out_ref, lst_i, lst_g, si, sg, sem):
    me = lax.axis_index("dp")
    rows = out_ref.shape[0]
    n_row = l_ref.shape[0]
    base = me * rows
    out_ref[...] = de_ref[...]
    yl = jnp.concatenate([jnp.sum(y_ref[r // NY, r % NY, :, 0, :], axis=0, keepdims=True) for r in range(n_row)], axis=0) - base
    own = (yl >= 0) & (yl < rows)
    g = jnp.where(own, (jnp.exp(jnp.where(own, z_ref[...], 0.0) - l_ref[...]) - 1.0) * (1.0 / (NZ * CH)), 0.0)
    of = jnp.where(own, 1.0, 0.0)
    tri = jnp.where(lax.broadcasted_iota(jnp.int32, (LANES, LANES), 0) < lax.broadcasted_iota(jnp.int32, (LANES, LANES), 1), 1.0, 0.0).astype(jnp.bfloat16)
    pre = jnp.dot(of.astype(jnp.bfloat16), tri, preferred_element_type=jnp.float32)
    tot = jnp.broadcast_to(jnp.sum(of, axis=1, keepdims=True), (n_row, LANES))
    low = jnp.where(lax.broadcasted_iota(jnp.int32, (n_row, n_row), 1) < lax.broadcasted_iota(jnp.int32, (n_row, n_row), 0), 1.0, 0.0).astype(jnp.bfloat16)
    off = jnp.dot(low, tot.astype(jnp.bfloat16), preferred_element_type=jnp.float32)
    rank = jnp.where(own, pre + off, -1.0)
    n = jnp.sum(of).astype(jnp.int32)
    lane = lax.broadcasted_iota(jnp.int32, (1, LANES), 1)

    def page(p, _):
        slot = (lax.broadcasted_iota(jnp.int32, (LANES, LANES), 0) + p * LANES).astype(jnp.float32)
        code = jnp.zeros((LANES, LANES), jnp.float32)
        gg = jnp.zeros((LANES, LANES), jnp.float32)
        tt = jnp.zeros((LANES, LANES), jnp.float32)
        for r in range(n_row):
            hit = rank[r:r + 1] == slot
            code += jnp.where(hit, yl[r:r + 1].astype(jnp.float32), 0.0)
            tt += jnp.where(hit, (lane + r * LANES).astype(jnp.float32), 0.0)
            gg += jnp.where(hit, g[r:r + 1], 0.0)
        row = lambda a: jnp.transpose(jnp.broadcast_to(jnp.sum(a, axis=1, keepdims=True), (LANES, LANES)))[:8]
        lst_i[0] = row(code).astype(jnp.int32)
        lst_i[1] = row(tt).astype(jnp.int32)
        lst_g[...] = row(gg)
        ca = pltpu.make_async_copy(lst_i, si, sem.at[0])
        cb = pltpu.make_async_copy(lst_g, sg, sem.at[1])
        ca.start()
        cb.start()
        ca.wait()
        cb.wait()

        def one(i, _):
            r, t, gv = si[0, 0, i], si[1, 0, i], sg[0, i]
            q, w = t // CHIP_TOK, t % CHIP_TOK
            hs = pl.ds(pl.multiple_of((w // DEV_TOK) * DEV_TOK, DEV_TOK), DEV_TOK)
            zz, yy, xx = q // (NY * NX), (q // NX) % NY, q % NX
            ht = jnp.concatenate([h_ref[0, zz, yy, xx, hs, :], h_ref[1, zz, yy, xx, hs, :]], axis=1).astype(jnp.float32)
            hr = jnp.sum(jnp.where(lax.broadcasted_iota(jnp.int32, (DEV_TOK, 1), 0) == w % DEV_TOK, ht, 0.0), axis=0, keepdims=True)
            out_ref[pl.ds(r, 1), :] += gv * hr
            return 0
        lax.fori_loop(0, jnp.minimum(n - p * LANES, LANES), one, 0)
        return 0
    lax.fori_loop(0, (n + 127) // LANES, page, 0)


def fix(de, hfull, yfull, lrow, zrow):
    V = pl.BlockSpec(memory_space=pltpu.VMEM)
    return pl.pallas_call(
        fix_kernel, name="fix", out_shape=jax.ShapeDtypeStruct(de.shape, jnp.float32),
        in_specs=[V] * 5, out_specs=V,
        scratch_shapes=[pltpu.VMEM((2, 8, LANES), jnp.int32), pltpu.VMEM((8, LANES), jnp.float32), pltpu.SMEM((2, 8, LANES), jnp.int32),
                        pltpu.SMEM((8, LANES), jnp.float32), pltpu.SemaphoreType.DMA((2,))],
        compiler_params=pltpu.CompilerParams(vmem_limit_bytes=40 * MIB),
    )(de, hfull, yfull, lrow, zrow)


def solution(mesh):
    def local_step(features, w_in, w_out, table_blk, cand_ids, log_q, targets):
        z, y, x, c = coords()
        pre_act = jnp.dot(features, w_in, preferred_element_type=jnp.float32)
        act_b = jax.nn.gelu(pre_act).astype(jnp.bfloat16)
        query = jnp.dot(act_b, w_out, preferred_element_type=jnp.float32).astype(jnp.bfloat16)
        yrow = lax.dynamic_update_slice(jnp.zeros((1, LANES), jnp.int32), targets[None, :], (0, CHIP_TOK * x + DEV_TOK * c))
        hfull, yfull = all_gather_y(query, yrow, 0, "ag_query")
        e, mcol, mrow, srow, zrow = scores(hfull, table_blk, yfull, cand_ids, log_q)
        lrow, loss = stats(mrow, srow, zrow, 1)
        dhfull, de = grads(e, mcol, hfull, table_blk, yfull, lrow, zrow, 2)
        grad_blk = fix(de, hfull, yfull, lrow, zrow)
        xfull = all_gather(features, 3, "ag_feat")
        dh = ag_rows(dhfull)
        feat = ag_rows(xfull)
        pre, = [jnp.dot(feat, w_in, preferred_element_type=jnp.float32)]
        act, back = jax.vjp(jax.nn.gelu, pre)
        act_all = act.astype(jnp.bfloat16)
        d_act = jnp.einsum("td,fd->tf", dh, w_out, preferred_element_type=jnp.float32)
        d_pre = back(d_act)[0].astype(jnp.bfloat16)
        grad_w_out = jnp.einsum("tf,td->fd", act_all, dh, preferred_element_type=jnp.float32)
        grad_w_in = jnp.einsum("ti,tf->if", feat, d_pre, preferred_element_type=jnp.float32)
        return loss[0, 0], grad_blk, grad_w_in, grad_w_out

    return jax.shard_map(local_step, mesh=mesh, in_specs=(P("dp", None), P(), P(), P("dp", None), P(), P(), P("dp")), out_specs=(P(), P("dp", None), P(), P()), check_vma=False)
```

time: 1980 us -> 279 us (0.14)
  waiting for transfers between devices: 1490 us -> 0 us
  blocking collectives: 304 us -> 0 us
  Pallas kernels: 0 us -> 215 us
  other arithmetic: 82.3 us -> 0 us
  local copies, waits for them, and re-layouts: 40.8 us -> 15.4 us
    reduce_scatter x1 -> x0, waiting for transfers between devices: 1280 us -> none  [local_step(): lax.psum_scatter(dq_part, 'dp', scatter_dimension=0, tiled=True)]
    psum x1 -> x0, waiting for transfers between devices: 216 us -> none  [local_step(): lax.psum(jnp.einsum('ti,tf->if', features, d_pre, preferred_element_type=...]
    pallas_call x0 -> x6, Pallas kernels: none -> 215 us  [the longest x1 68.1 us: grads(): pl.pallas_call(grad_kernel, name='grads', out_shape=(jax.ShapeDtypeStruct...]
    psum x2 -> x0, blocking collectives: 150 us -> none  [the longest x1 76 us: local_step(): tgt_logit = lax.psum(jnp.where(tgt_own, tgt_dot, 0.0), 'dp')]
    unnamed x1 -> x0, blocking collectives: 81.9 us -> none
    pmax x1 -> x0, blocking collectives: 72.7 us -> none  [local_step(): lax.pmax(jnp.max(cand_logit, axis=1), 'dp')]
    scatter-add x2 -> x0, other arithmetic: 46.7 us -> none  [local_step(): jnp.zeros(table_blk.shape, jnp.float32).at[cand_index].add(grad_cand)]
    gather x2 -> x0, local copies, waits for them, and re-layouts: 26.1 us -> none  [the longest x1 17 us: local_step(): tgt_rows = table_blk[tgt_index]]
  transfers between devices with their start and end apart: 3 -> 0, of which waited for: 2 -> 0; matrix products, arithmetic and copies ran while one was open for 4% -> 0% of each run, Pallas kernels for 0% -> 0%
where the time goes in v1:
time: 279 us
  Pallas kernels  215 us (77%)
  matrix products  48 us (17%)
  local copies, waits for them, and re-layouts  15.4 us (6%)
    pallas_call x1, Pallas kernels, grads(): pl.pallas_call(grad_kernel, name='grads', out_shape=(jax.ShapeDtypeStruct...  68.1 us
    pallas_call x1, Pallas kernels, all_gather(): pl.pallas_call(ag_kernel, name=name, out_shape=jax.ShapeDtypeStruct((2, N...  54.2 us
    pallas_call x1, Pallas kernels, all_gather_y(): pl.pallas_call(ag_y_kernel, name=name, out_shape=(jax.ShapeDtypeStruct((2...  45.7 us
    dot_general x1, matrix products, local_step(): jnp.einsum('ti,tf->if', feat, d_pre, preferred_element_type=jnp.float32)  24.3 us
    pallas_call x1, Pallas kernels, stats(): pl.pallas_call(stats_kernel, name='stats', out_shape=(jax.ShapeDtypeStruc...  21.1 us
    pallas_call x1, Pallas kernels, scores(): pl.pallas_call(scores_kernel, name='scores', grid=(NZ,), out_shape=(jax.S...  21.1 us
    unnamed x38, local copies, waits for them, and re-layouts  12.4 us
    dot_general x1, matrix products, local_step(): pre, = [jnp.dot(feat, w_in, preferred_element_type=jnp.float32)]  11.7 us

profile of v1, /device:TPU:1, one launch (start us, length us, event | category | flops | bytes accessed | tf_op | source)
XLA Modules:
  0.0 278.8 jit_solution(16944689818661515170)
XLA Ops:
  0.6 0.0 copy-start
  0.6 1.6 copy-done
  2.2 1.6 convolution_convert_fusion.src_ref
  3.9 0.9 dynamic_update_slice.3.y_ref
  4.7 45.7 %ag_query.1 = (bf16[2,8,4,4,32,128]{5,4,3,2,1,0:T(8,128)(2,1)S(1)}, s32[8,4,4,1,128]{4,3,2,1,0:T(1,128)S(1)}) custom-call(bf16[16,256]{1,0:T(8,128)(2,1)S(1)} %convolution_convert_fusion.src_ref, s32[1,128]{1,0:T(1,128)S(1)} %dynamic_update_slice.3.y_ref), custom_call_target="tpu_custom_call" | custom-call | tf_op jit(solution)/shard_map/ag_query/pallas_call | solution.py:152
  50.4 0.0 copy-start.7
  50.5 0.0 copy-start.4
  50.5 1.2 copy-done.4
  51.7 21.1 %scores.1 = (f32[4096,2048]{1,0:T(8,128)}, f32[4096,128]{1,0:T(8,128)S(1)}, f32[32,128]{1,0:T(8,128)S(1)}, f32[32,128]{1,0:T(8,128)S(1)}, f32[32,128]{1,0:T(8,128)S(1)}) custom-call(bf16[2,8,4,4,32,128]{5,4,3,2,1,0:T(8,128)(2,1)S(1)} %get-tuple-element.15.h_ref, bf16[2048,256]{1,0:T(8,128)(2,1)S(1)} %copy-done.4, ...), custom_call_target="tpu_custom_call" | custom-call | tf_op jit(solution)/shard_map/scores/pallas_call | solution.py:263
  72.8 0.0 copy-start.2
  72.8 1.3 copy-done.2
  74.2 0.0 copy-start.5
  74.2 1.3 copy-done.5
  75.5 0.0 copy-start.9
  75.5 0.6 copy-done.9
  76.1 0.0 copy-start.13
  76.1 0.6 copy-done.13
  76.7 0.0 copy-start.14
  76.7 0.6 copy-done.14
  77.3 21.1 %stats.1 = (f32[32,128]{1,0:T(8,128)}, f32[8,128]{1,0:T(8,128)}) custom-call(f32[32,128]{1,0:T(8,128)} %copy-done.13, f32[32,128]{1,0:T(8,128)} %copy-done.14, f32[32,128]{1,0:T(8,128)} %copy-done.9), custom_call_target="tpu_custom_call" | custom-call | tf_op jit(solution)/shard_map/stats/pallas_call | solution.py:341
  98.4 1.2 slice.15
  99.6 0.0 copy-done.7
  99.6 0.0 copy-start.10
  99.6 0.0 copy-start.12
  99.6 0.0 copy-start.11
  99.6 68.1 %grads.1 = (bf16[2,8,4,4,32,128]{5,4,3,2,1,0:T(8,128)(2,1)}, f32[2048,256]{1,0:T(8,128)}) custom-call(f32[4096,2048]{1,0:T(8,128)} %get-tuple-element.21.e_hbm, f32[4096,128]{1,0:T(8,128)} %copy-done.5, bf16[2,8,4,4,32,128]{5,4,3,2,1,0:T(8,128)(2,1)} %copy-done.2, bf16[2048,256]{1,0:T(8,128)(2,1)} %emb_ref.3, s32[8,4,4,1,128]{4,3,2,1,0:T(1,128)} %copy-done.7, ...), custom_call_target="tpu_custom_call" | custom-call | tf_op jit(solution)/shard_map/grads/pallas_call | solution.py:475
  167.7 0.0 copy-done.10
  167.7 0.0 copy-done.12
  167.7 0.0 copy-start.3
  167.7 1.6 copy-done.3
  169.3 0.0 copy-start.6
  169.3 1.6 copy-done.6
  170.9 0.0 copy-start.8
  170.9 0.8 copy-done.8
  171.7 4.4 %fix.1 = f32[2048,256]{1,0:T(8,128)} custom-call(f32[2048,256]{1,0:T(8,128)S(1)} %copy-done.6, bf16[2,8,4,4,32,128]{5,4,3,2,1,0:T(8,128)(2,1)S(1)} %copy-done.3, s32[8,4,4,1,128]{4,3,2,1,0:T(1,128)S(1)} %copy-done.8, f32[32,128]{1,0:T(8,128)S(1)} %copy-done.12, f32[32,128]{1,0:T(8,128)S(1)} %copy-done.10), custom_call_target="tpu_custom_call" | custom-call | tf_op jit(solution)/shard_map/fix/pallas_call | solution.py:545
  176.1 0.0 copy-done.11
  176.1 54.2 %ag_feat.1 = bf16[2,8,4,4,32,512]{5,4,3,2,1,0:T(8,128)(2,1)S(1)} custom-call(bf16[16,1024]{1,0:T(8,128)(2,1)S(1)} %copy-done.11), custom_call_target="tpu_custom_call" | custom-call | tf_op jit(solution)/shard_map/ag_feat/pallas_call | solution.py:139
  230.3 0.7 fusion.44
  231.0 0.0 copy-start.15
  231.0 0.0 copy-start.16
  231.0 0.0 copy-start.17
  231.0 11.7 %fusion.10 = f32[4096,1024]{1,0:T(8,128)} fusion(bf16[1024,1024]{1,0:T(8,128)(2,1)S(1)} %copy-done, bf16[4096,512]{1,0:T(8,128)(2,1)S(1)} %bitcast.15, bf16[4096,512]{1,0:T(8,128)(2,1)S(1)} %bitcast.13), kind=kOutput, calls=%fused_computation.13 | convolution fusion | flops 8606711808 | bytes 27262976 | tf_op jit(solution)/shard_map/dot_general | solution.py:569
  242.8 0.0 copy-done.15
  242.8 0.0 copy-done.16
  242.8 0.0 copy-done.17
  242.8 0.4 fusion.45
  243.2 0.0 copy-start.18
  243.2 1.0 copy-done.18
  244.2 24.3 %fusion.8 = f32[1024,1024]{1,0:T(8,128)} fusion(f32[4096,1024]{1,0:T(8,128)} %fusion.10, bf16[4096,512]{1,0:T(8,128)(2,1)} %bitcast.16, bf16[4096,512]{1,0:T(8,128)(2,1)} %bitcast.14, bf16[1024,256]{1,0:T(8,128)(2,1)} %param.9, bf16[4096,128]{1,0:T(8,128)(2,1)S(1)} %bitcast.21, bf16[4096,128]{1,0:T(8,128)(2,1)S(1)} %bitcast.19), kind=kOutput, calls=%fused_computation.12 | convolution fusion | flops 10842275840 | bytes 31981568 | tf_op jit(solution)/shard_map/ti,tf->if/dot_general | solution.py:575
  268.5 0.0 copy-start.1
  268.5 10.3 %fusion.7 = f32[1024,256]{1,0:T(8,128)} fusion(f32[4096,1024]{1,0:T(8,128)} %fusion.10, bf16[4096,128]{1,0:T(8,128)(2,1)} %bitcast.22, bf16[4096,128]{1,0:T(8,128)(2,1)S(1)} %bitcast.20), kind=kOutput, calls=%fused_computation.11 | convolution fusion | flops 2189426688 | bytes 19922944 | tf_op jit(solution)/shard_map/tf,td->fd/dot_general | solution.py:574
  278.8 0.0 copy-done.1
  (1 shorter events, 0.0 us)
Async XLA Ops:
  0.6 1.6 copy-start
  50.4 49.2 %copy-start.7 = (s32[8,4,4,1,128]{4,3,2,1,0:T(1,128)}, s32[8,4,4,1,128]{4,3,2,1,0:T(1,128)S(1)}, u32[]{:S(2)}) copy-start(s32[8,4,4,1,128]{4,3,2,1,0:T(1,128)S(1)} %get-tuple-element.16.y_ref) | copy-start | bytes 196612
  50.5 1.3 copy-start.4
  72.8 1.3 copy-start.2
  74.2 1.3 copy-start.5
  75.5 0.6 copy-start.9
  76.1 0.6 copy-start.13
  76.7 0.6 copy-start.14
  99.6 68.1 %copy-start.10 = (f32[32,128]{1,0:T(8,128)S(1)}, f32[32,128]{1,0:T(8,128)}, u32[]{:S(2)}) copy-start(f32[32,128]{1,0:T(8,128)} %copy-done.9) | copy-start | bytes 49156
  99.6 68.1 %copy-start.12 = (f32[32,128]{1,0:T(8,128)S(1)}, f32[32,128]{1,0:T(8,128)}, u32[]{:S(2)}) copy-start(f32[32,128]{1,0:T(8,128)} %get-tuple-element.23.l_ref) | copy-start | bytes 49156
  99.6 76.5 %copy-start.11 = (bf16[16,1024]{1,0:T(8,128)(2,1)S(1)}, bf16[16,1024]{1,0:T(8,128)(2,1)}, u32[]{:S(2)}) copy-start(bf16[16,1024]{1,0:T(8,128)(2,1)} %src_ref.1) | copy-start | bytes 98308
  167.7 1.6 copy-start.3
  169.3 1.6 copy-start.6
  170.9 0.8 copy-start.8
  231.0 11.8 %copy-start.15 = (bf16[1,8,4,4,32,512]{5,4,3,2,1,0:T(8,128)(2,1)}, bf16[1,8,4,4,32,512]{5,4,3,2,1,0:T(8,128)(2,1)S(1)}, u32[]{:S(2)}) copy-start(bf16[1,8,4,4,32,512]{5,4,3,2,1,0:T(8,128)(2,1)S(1)} %get-tuple-element.26) | copy-start | bytes 12582916
  231.0 11.8 %copy-start.16 = (bf16[1,8,4,4,32,512]{5,4,3,2,1,0:T(8,128)(2,1)}, bf16[1,8,4,4,32,512]{5,4,3,2,1,0:T(8,128)(2,1)S(1)}, u32[]{:S(2)}) copy-start(bf16[1,8,4,4,32,512]{5,4,3,2,1,0:T(8,128)(2,1)S(1)} %get-tuple-element.27) | copy-start | bytes 12582916
  231.0 11.8 %copy-start.17 = (bf16[2,8,4,4,32,128]{5,4,3,2,1,0:T(8,128)(2,1)S(1)}, bf16[2,8,4,4,32,128]{5,4,3,2,1,0:T(8,128)(2,1)}, u32[]{:S(2)}) copy-start(bf16[2,8,4,4,32,128]{5,4,3,2,1,0:T(8,128)(2,1)} %get-tuple-element.25) | copy-start | bytes 6291460
  243.2 1.1 copy-start.18
  268.5 10.3 %copy-start.1 = (bf16[1024,1024]{1,0:T(8,128)(2,1)S(1)}, bf16[1024,1024]{1,0:T(8,128)(2,1)}, u32[]{:S(2)}) copy-start(bf16[1024,1024]{1,0:T(8,128)(2,1)} %param.8) | copy-start | bytes 6291460

commit v2 on v0

v2 whole, which is shorter than its diff:
```python
import functools
import math
import jax
import jax.numpy as jnp
from jax import lax
from jax.experimental import pallas as pl
from jax.experimental.pallas import tpu as pltpu
from jax.sharding import PartitionSpec as P

NZ, NY, NX = 8, 4, 4
NA = 4
LN = 128
TD = 16
NC = 2 * NA
CH = NZ * NA * TD
NT = NC * CH
PZ = NA * TD
SR = NT // LN
GR = CH // LN
F32, BF16 = jnp.float32, jnp.bfloat16
NEG = -jnp.inf
MESH = pl.DeviceIdType.MESH
DMA = pltpu.SemaphoreType.DMA


def coords():
    me = lax.axis_index("dp")
    z, y, x, c = me // (NY * NX * 2), (me // (NX * 2)) % NY, (me // 2) % NX, me % 2
    return z, y, x, c, x * (1 - c) + y * c, y * (1 - c) + x * c


def dev(z, y, x, c):
    return (((z * NY + y) * NX + x) * 2 + c,)


def peers():
    z, y, x, c, v, a = coords()
    return (dev(z, y, x, 1 - c), lambda k: dev((z + k) % NZ, y, x, c), lambda k: dev(z, (y + k * c) % NY, (x + k * (1 - c)) % NX, c),
            lambda k: dev(z, (y + k * (1 - c)) % NY, (x + k * c) % NX, c))


def rcopy(src, dst, ssem, rsem, to):
    return pltpu.make_async_remote_copy(src_ref=src, dst_ref=dst, send_sem=ssem, recv_sem=rsem, device_id=to, device_id_type=MESH)


def run(copies):
    for cp in copies:
        cp.start()
    for cp in copies:
        cp.wait()


def signal_peers():
    bar = pltpu.get_barrier_semaphore()
    to_c, to_z, to_1, to_2 = peers()
    everyone = [to_c] + [to_1(k) for k in range(1, NA)] + [to_2(k) for k in range(1, NA)] + [to_z(k) for k in range(1, NZ)]
    for p in everyone:
        pl.semaphore_signal(bar, inc=1, device_id=p, device_id_type=MESH)
    return bar, len(everyone)


NEAR = (1, 3, 2)


class Gather:
    SEMS = [DMA((NZ - 1,)), DMA((NZ - 1,)), DMA((NA,)), DMA((NA,)), DMA((NA, NA)), DMA((NA, NA)), DMA((NA,)), DMA((NA,))]

    def __init__(self, buf, sems, src=None):
        z, y, x, c, v, a = coords()
        sz, rz, s2, r2, s1, r1, sd, rd = sems
        to_c, to_z, to_1, to_2 = peers()
        self.c, self.v, self.a = c, v, a
        own = buf.at[c, v, z, a]
        col = lambda j: buf.at[c, v, :, (a + NA - j) % NA]
        chunk = lambda j: buf.at[c, (v + NA - j) % NA]
        self.zc = lambda k: rcopy(own if src is None else src, own, sz.at[k - 1], rz.at[k - 1], to_z(k))
        self.ac = lambda k: rcopy(col(0), col(0), s2.at[k], r2.at[k], to_2(k))
        self.vc = lambda k, p: rcopy(col(p), col(p), s1.at[k, p], r1.at[k, p], to_1(k))
        self.dc = lambda j: rcopy(chunk(j), chunk(j), sd.at[j], rd.at[j], to_c)

    def start(self):
        @pl.loop(1, NZ)
        def _(k):
            self.zc(k).start()

    def second(self):
        @pl.loop(1, NZ)
        def _(k):
            self.zc(k).wait()
        for k in NEAR:
            self.ac(k).start()

    def first(self):
        for k in NEAR:
            self.vc(k, 0).start()
        for j in NEAR:
            self.ac(j).wait()
            for k in NEAR:
                self.vc(k, j).start()
        self.dc(0).start()

    def take(self, n):
        i, p = n // 2, n % 2
        j = i + (i // 2) * (1 - 2 * (i % 2))

        @pl.when((p == 0) & (i > 0))
        def _():
            for q in range(NA):
                self.vc(j, q).wait()
            self.dc(j).start()

        @pl.when(p == 1)
        def _():
            self.dc(j).wait()
        return self.c + p * (1 - 2 * self.c), (self.v * (1 - p) + self.a * p + NA - j) % NA


def to_col(row):
    return jnp.transpose(jnp.broadcast_to(row, (LN, LN)))


def logq_rows(cid_v, lq_v, lqr_ref, base):
    @pl.loop(0, lqr_ref.shape[1] // LN)
    def _(i):
        blk = pl.multiple_of(i * LN, LN)
        rid = lax.broadcasted_iota(jnp.int32, (LN, LN), 0) + (base + blk)
        acc = jnp.zeros((LN, LN), F32)
        for q in range(cid_v.shape[0]):
            acc += jnp.where(cid_v[q:q + 1, :] == rid, lq_v[q:q + 1, :], 0.0)
        lqr_ref[:, pl.ds(blk, LN)] = jnp.transpose(jnp.broadcast_to(jnp.sum(acc, axis=1, keepdims=True), (LN, LN)))[:8]


def target_cols(yblk, base, yl_ref, row, d_ref):
    lane = lax.broadcasted_iota(jnp.int32, (LN, LN), 1).astype(F32)
    group = lax.broadcasted_iota(jnp.int32, (1, LN), 1) // TD
    for g in range(GR):
        yr = sum(jnp.where(group == b, yblk(g * 8 + b), 0) for b in range(8)) - base
        yl_ref[pl.ds(row + g, 1), :] = yr
        d_ref[g * LN:(g + 1) * LN, :] = to_col(yr.astype(F32)) - lane


def scores_chunk(h, emb_ref, lqr_ref, e_ref, d_ref, mcol_ref, zcol_ref, scol_ref):
    rows = emb_ref.shape[0]
    RB = PZ
    for j in range(0, rows, 2 * LN):
        s = lax.dot_general(h, emb_ref[j:j + 2 * LN, :], (((1,), (1,)), ((), ())), preferred_element_type=F32)
        for rb in range(0, CH, RB):
            rs = slice(rb, rb + RB)
            m = mcol_ref[rs, :] if j else jnp.full((RB, LN), NEG, F32)
            zc = zcol_ref[rs, :] if j else jnp.full((RB, LN), NEG, F32)
            d = d_ref[rs, :]
            for k in (0, LN):
                raw = s[rs, k:k + LN]
                hit = d == float(j + k)
                zc = jnp.where(hit, raw, zc)
                val = jnp.where(hit, -1e9, raw - lqr_ref[:1, j + k:j + k + LN])
                e_ref[rs, j + k:j + k + LN] = val
                m = jnp.maximum(m, val)
            mcol_ref[rs, :] = m
            zcol_ref[rs, :] = zc
    for rb in range(0, CH, RB):
        rs = slice(rb, rb + RB)
        zc = jnp.max(zcol_ref[rs, :], axis=1, keepdims=True)
        m = jnp.maximum(jnp.max(mcol_ref[rs, :], axis=1, keepdims=True), zc)
        zcol_ref[rs, :] = jnp.broadcast_to(zc, (RB, LN))
        mcol_ref[rs, :] = jnp.broadcast_to(m, (RB, LN))

    def grp(g, _):
        rs = pl.ds(pl.multiple_of(g * 2 * TD, 2 * TD), 2 * TD)
        m = mcol_ref[rs, :]
        tot = jnp.zeros((2 * TD, LN), F32)
        for k in range(0, rows, LN):
            ex = jnp.exp(e_ref[rs, k:k + LN] - m)
            e_ref[rs, k:k + LN] = ex
            tot += ex
        scol_ref[rs, :] = tot
        return 0
    lax.fori_loop(0, CH // (2 * TD), grp, 0)
    for rb in range(0, CH, RB):
        rs = slice(rb, rb + RB)
        tot = jnp.sum(scol_ref[rs, :], axis=1, keepdims=True)
        scol_ref[rs, :] = jnp.broadcast_to(tot, (RB, LN)) + jnp.exp(zcol_ref[rs, :] - mcol_ref[rs, :])


HR = SR // 2


def merge_stats(parts):
    m = functools.reduce(jnp.maximum, [p[:HR] for p in parts])
    s = sum(p[HR:2 * HR] * jnp.exp(p[:HR] - m) for p in parts)
    return m, s, sum(p[2 * HR:] for p in parts)


def put_stats(ref, parts):
    m, s, t = merge_stats(parts)
    ref[:HR, :] = m
    ref[HR:2 * HR, :] = s
    ref[2 * HR:, :] = t


def reduce_stats(mr, sr, zr, lr, b0, bc, b1, bs, b2, bz, fin, sems, fill):
    z, y, x, c, v, a = coords()
    to_c, to_z, to_1, to_2 = peers()
    sc, rc, s1, r1, ss, rs, s2, r2, sz, rz, sf, rf = sems

    def step(copies, lo=0, hi=0):
        for cp in copies:
            cp.start()
        if hi:
            fill(lo, hi)
        for cp in copies:
            cp.wait()
    for hf in range(2):
        hs = slice(hf * HR, (hf + 1) * HR)
        zz = zr[hs, :]
        zz = jnp.where(zz > NEG, zz, 0.0)
        b0[hf, :HR, :] = mr[hs, :]
        b0[hf, HR:2 * HR, :] = sr[hs, :]
        b0[hf, 2 * HR:, :] = zz[:8] + zz[8:]
    step([rcopy(b0.at[1 - c], bc, sc, rc, to_c)])
    here, there = b0[c], bc[...]
    even = c == 0
    put_stats(b1.at[a], [jnp.where(even, here, there), jnp.where(even, there, here)])
    step([rcopy(b1.at[a], b1.at[a], s1.at[k], r1.at[k], to_2(k)) for k in NEAR], 0, 2)
    put_stats(b0.at[c], [b1[i] for i in range(NA)])
    step([rcopy(b0.at[c], bs, ss, rs, to_c)])
    b2[a] = bs[...]
    step([rcopy(bs, b2.at[a], s2.at[k], r2.at[k], to_2(k)) for k in NEAR], 2, 5)
    put_stats(bz.at[z], [b2[i] for i in range(NA)])
    step([rcopy(bz.at[z], bz.at[z], sz.at[k - 1], rz.at[k - 1], to_z(k)) for k in range(1, NZ)], 5, NC)
    m, s, t = merge_stats([bz[i] for i in range(NZ)])
    fin[1 - c, :HR, :] = m + jnp.log(s)
    fin[1 - c, HR:, :] = t
    step([rcopy(fin.at[1 - c], fin.at[1 - c], sf, rf, to_c)])
    tot = fin[0, :HR, :] + fin[1, :HR, :]
    tot = tot[:8] + tot[8:] - (fin[0, HR:, :] + fin[1, HR:, :])
    lr[:HR, :] = fin[0, :HR, :]
    lr[HR:, :] = fin[1, :HR, :]
    return jnp.sum(tot) * (1.0 / NT)


def gelu_both(u):
    k0, k1 = math.sqrt(2.0 / math.pi), 0.044715
    sq = u * u
    t = jnp.tanh(k0 * (u + k1 * (sq * u)))
    cdf = 0.5 * (1.0 + t)
    return u * cdf, cdf + (0.5 * k0) * u * ((1.0 - t * t) * (1.0 + (3.0 * k1) * sq))


def step_kernel(x_hbm, win_hbm, wout_hbm, emb_hbm, cid_hbm, lq_hbm, y_s,
                loss_ref, de_hbm, gwi_hbm, gwo_hbm, h_hbm, yl_out, l_out, z_out, xg,
                xv, win, wout, emb, cid_v, lq_v, lqr, hb, yb, dh,
                eb, pb, de, te, dcol, mcol, zcol, scol, mr, sr, zr, yl,
                b0, bc, b1, bs, b2, bz, fin,
                dq, rc, a0, ra, a1, rb, zb,
                lsem, osem, fsem, xsem, *sems):
    z, y, x, c, v, a = coords()
    to_c, to_z, to_1, to_2 = peers()
    rows = emb.shape[0]
    hid = win.shape[1]
    half = hid // 2
    me = lax.axis_index("dp")
    base = me * rows
    gh, gy, gx, gd, sems = sems[:8], sems[8:16], sems[16:24], sems[24:32], sems[32:]
    own16 = pl.ds(me * TD, TD)
    loads = [pltpu.make_async_copy(s, d, lsem.at[i]) for i, (s, d) in enumerate((
        (x_hbm, xv), (win_hbm, win), (wout_hbm, wout), (emb_hbm, emb), (cid_hbm.at[own16], cid_v), (lq_hbm.at[own16], lq_v)))]
    for cp in loads:
        cp.start()
    bar, n_peers = signal_peers()

    for cp in loads[:3]:
        cp.wait()
    pre = jnp.dot(xv[...], win[...], preferred_element_type=F32)
    act = gelu_both(pre)[0].astype(BF16)
    hb[c, v, z, a] = jnp.dot(act, wout[...], preferred_element_type=F32).astype(BF16)
    lane16 = lax.broadcasted_iota(jnp.int32, (1, LN), 1) % TD
    yb[c, v, z, a] = sum(jnp.where(lane16 == i, y_s[i], 0) for i in range(TD))
    xown = pltpu.make_async_copy(xv, xg.at[c, v, z, a], xsem.at[0])
    xown.start()
    pl.semaphore_wait(bar, n_peers)

    gath, gaty, gatx, gatd = Gather(hb, gh), Gather(yb, gy), Gather(xg, gx, xv), Gather(dh, gd)
    gath.start()
    gaty.start()
    gatx.start()
    for cp in loads[3:]:
        cp.wait()
    logq_rows(cid_v, lq_v, lqr, base)
    de[...] = jnp.zeros_like(de)
    for g in (gath, gaty):
        g.second()
    for g in (gath, gaty):
        g.first()
    xown.wait()
    gatx.second()

    def score(cc, vv):
        ci = cc * NA + vv
        target_cols(lambda b: yb[cc, vv, b // NA, b % NA], base, yl, ci * GR, dcol.at[ci])
        scores_chunk(hb[cc, vv].reshape(CH, 2 * LN), emb, lqr, eb.at[ci], dcol.at[ci], mcol.at[ci], zcol.at[ci], scol)
        for b in range(GR):
            bs_ = slice(b * LN, (b + 1) * LN)
            row = pl.ds(ci * GR + b, 1)
            mr[row, :] = jnp.transpose(mcol[ci, bs_, :])[:1]
            sr[row, :] = jnp.transpose(scol[bs_, :])[:1]
            zr[row, :] = jnp.transpose(zcol[ci, bs_, :])[:1]

    @pl.loop(0, NC)
    def _(n):
        gaty.take(n)
        score(*gath.take(n))
        pl.when(n == NA - 1)(gatx.first)

    def target_rows(lo, hi):
        @pl.loop(lo, hi)
        def _(ci):
            for q in range(0, rows, LN):
                pb[:, q:q + LN] = jnp.where(dcol[ci] == float(q), 1.0, 0.0).astype(BF16)
            te[ci] = jnp.dot(pb[...], emb[...], preferred_element_type=F32).astype(BF16)

    lr = l_out
    loss_ref[0, 0] = reduce_stats(mr, sr, zr, lr, b0, bc, b1, bs, b2, bz, fin, sems[:12], target_rows)
    @pl.loop(0, NC)
    def _(ci):
        for b in range(GR):
            bs_ = slice(b * LN, (b + 1) * LN)
            lc = to_col(lr[pl.ds(ci * GR + b, 1), :])
            mcol[ci, bs_, :] = jnp.exp(mcol[ci, bs_, :] - lc) * (1.0 / NT)
            zc = zcol[ci, bs_, :]
            zcol[ci, bs_, :] = jnp.where(zc > NEG, (jnp.exp(zc - lc) - 1.0) * (1.0 / NT), 0.0)
    yl_out[...] = yl[...]
    z_out[...] = zr[...]

    sc, rcs, sa, ras, sb, rbs, sz, rzs = sems[12:20]
    ring = a0.shape[0]
    c_copy = lambda k: rcopy(dq.at[k % 2, 1 - c], rc.at[k], sc.at[k], rcs.at[k], to_c)
    a_copy = lambda k, j: rcopy(a0.at[k % ring, (v + j) % NA], ra.at[k, v], sa.at[k, j], ras.at[k, j], to_1(j))
    b_copy = lambda k, j: rcopy(a1.at[k % ring, (a + j) % NA], rb.at[k, a], sb.at[k, j], rbs.at[k, j], to_2(j))

    def off(k):
        s = (k + 1) // 2
        return NA + s - 2 * s * (k % 2)

    z_copy = lambda k: rcopy(zb.at[NZ + k], zb.at[z], sz.at[k], rzs.at[k], to_z(off(k)))

    def compute(k):
        zz = (z + off(k)) % NZ
        piece = pl.ds(pl.multiple_of(zz * PZ, PZ), PZ)
        for ci in range(NC):
            ps = slice(ci * PZ, (ci + 1) * PZ)
            f = mcol[ci, piece, :]
            for q in range(0, rows, LN):
                pb[ps, q:q + LN] = (eb[ci, piece, q:q + LN] * f).astype(BF16)
        h = jnp.concatenate([hb[ci // NA, ci % NA, zz].reshape(PZ, 2 * LN) for ci in range(NC)], axis=0)
        for q in range(0, rows, CH):
            de[q:q + CH, :] += lax.dot_general(pb[:, q:q + CH], h, (((0,), (0,)), ((), ())), preferred_element_type=F32)
        out = jnp.dot(pb[...], emb[...], preferred_element_type=F32)
        for ci in range(NC):
            g = zcol[ci, piece, :]
            t = te[ci, piece, :].astype(F32)
            for hf in (0, LN):
                dq[k % 2, ci // NA, ci % NA, :, hf:hf + LN] = out[ci * PZ:(ci + 1) * PZ, hf:hf + LN] + g * t[:, hf:hf + LN]
        c_copy(k).start()

    def sum_core(k):
        c_copy(k).wait()
        a0[k % ring] = dq[k % 2, c] + rc[k]
        for j in NEAR:
            a_copy(k, j).start()

    def sum_first(k):
        for j in NEAR:
            a_copy(k, j).wait()
        ra[k, v] = a0[k % ring, v]
        a1[k % ring] = ((ra[k, 0] + ra[k, 1]) + (ra[k, 2] + ra[k, 3])).reshape(NA, TD, 2 * LN)
        for j in NEAR:
            b_copy(k, j).start()

    def sum_second(k, last=False):
        for j in NEAR:
            b_copy(k, j).wait()
        rb[k, a] = a1[k % ring, a]
        val = (rb[k, 0] + rb[k, 1]) + (rb[k, 2] + rb[k, 3])
        if last:
            zb[z] = val
        else:
            zb[NZ + k] = val
            z_copy(k).start()

    def body(k, _):
        compute(k)
        for lag, f in ((1, sum_core), (3, sum_first), (5, sum_second)):
            pl.when(k >= lag)(functools.partial(f, k - lag))
        return 0

    lax.fori_loop(0, NZ, body, 0)
    outs = [pltpu.make_async_copy(de, de_hbm, osem.at[0]), pltpu.make_async_copy(hb, h_hbm, osem.at[1])]
    for cp in outs:
        cp.start()

    cols = pl.ds(pl.multiple_of(c * half, half), half)
    xs = lambda ci, slot: pltpu.make_async_copy(xg.at[ci // NA, ci % NA].reshape(CH, hid), pb.at[:, pl.ds(pl.multiple_of(slot * hid, hid), hid)], fsem.at[slot])

    def tower(ci, slot):
        pre = jnp.dot(pb[:, pl.ds(pl.multiple_of(slot * hid, hid), hid)], win[:, cols], preferred_element_type=F32)
        act, der = gelu_both(pre)
        eb[ci, :, :half] = der
        eb[ci, :, half:2 * half] = act.astype(BF16).astype(F32)

    sum_core(7)
    sum_first(5)
    sum_second(3)
    sum_first(6)
    sum_second(4)
    sum_second(5)
    sum_first(7)
    sum_second(6)
    sum_second(7, last=True)
    for k in range(NZ - 1):
        z_copy(k).wait()
    tot = ((zb[0] + zb[1]) + (zb[2] + zb[3])) + ((zb[4] + zb[5]) + (zb[6] + zb[7]))
    dh[c, v, z, a] = tot.astype(BF16)
    gatd.start()
    pl.loop(0, NC)(lambda n: gatx.take(n) and None)
    xs(0, 0).start()

    def towers(lo, hi):
        @pl.loop(lo, hi)
        def _(ci):
            @pl.when(ci + 1 < NC)
            def _():
                xs(ci + 1, (ci + 1) % 2).start()
            xs(ci, ci % 2).wait()
            tower(ci, ci % 2)

    towers(0, 3)
    gatd.second()
    towers(3, 5)
    gatd.first()
    towers(5, NC)

    acc_i, acc_o = eb.at[pl.ds(0, 2), :, pl.ds(2 * half, half)], eb.at[2, :, pl.ds(2 * half, 2 * LN)]
    acc_i[...] = jnp.zeros(acc_i.shape, F32)
    acc_o[...] = jnp.zeros(acc_o.shape, F32)

    def weights(ci, slot):
        g = dh[ci // NA, ci % NA].reshape(CH, 2 * LN)
        back = lax.dot_general(g, wout[cols, :], (((1,), (1,)), ((), ())), preferred_element_type=F32)
        da = (eb[ci, :, :half] * back).astype(BF16)
        act = eb[ci, :, half:2 * half].astype(BF16)
        acc_o[...] += lax.dot_general(act, g, (((0,), (0,)), ((), ())), preferred_element_type=F32)
        for r in range(2):
            xr = pb[:, pl.ds(pl.multiple_of(slot * hid + r * half, half), half)]
            acc_i[r] += lax.dot_general(xr, da, (((0,), (0,)), ((), ())), preferred_element_type=F32)

    @pl.loop(0, NC)
    def _(n):
        cc, vv = gatd.take(n)
        cp = xs(cc * NA + vv, n % 2)
        cp.start()
        cp.wait()
        weights(cc * NA + vv, n % 2)

    so, ro = sems[20:22]
    mine = [(acc_i.at[r], gwi_hbm.at[pl.ds(r * half, half), cols]) for r in range(2)] + [(acc_o, gwo_hbm.at[cols])]
    ends = [rcopy(s, d, so.at[i], ro.at[i], to_c) for i, (s, d) in enumerate(mine)]
    outs += [pltpu.make_async_copy(s, d, osem.at[2 + i]) for i, (s, d) in enumerate(mine)]
    for cp in ends + outs[2:]:
        cp.start()
    for cp in ends + outs:
        cp.wait()


def step(features, w_in, w_out, table, cand_ids, log_q, targets):
    rows, dim = table.shape
    hid = w_in.shape[1]
    V, A, S = (pl.BlockSpec(memory_space=m) for m in (pltpu.VMEM, pl.ANY, pltpu.SMEM))
    sds = jax.ShapeDtypeStruct
    vm = pltpu.VMEM
    tokens = (2, NA, NZ, NA, TD)
    stat = lambda *n: vm(n + (2 * HR + 8, LN), F32)
    col = vm((NC, CH, LN), F32)
    row = vm((SR, LN), F32)
    return pl.pallas_call(
        step_kernel, name="step",
        out_shape=(sds((1, 1), F32), sds((rows, dim), F32), sds((w_in.shape[0], hid), F32), sds((hid, dim), F32), sds(tokens + (dim,), BF16),
                   sds((SR, LN), jnp.int32), sds((SR, LN), F32), sds((SR, LN), F32), sds(tokens + (w_in.shape[0],), BF16)),
        in_specs=[A] * 6 + [S], out_specs=(S, A, A, A, A, V, V, V, A),
        scratch_shapes=[
            vm(features.shape, BF16), vm(w_in.shape, BF16), vm(w_out.shape, BF16), vm(table.shape, BF16), vm((TD, LN), jnp.int32), vm((TD, LN), F32),
            vm((8, rows), F32), vm(tokens + (dim,), BF16), vm((2, NA, NZ, NA, 1, LN), jnp.int32), vm(tokens + (dim,), BF16),
            vm((NC, CH, rows), F32), vm((CH, rows), BF16), vm((rows, dim), F32), vm((NC, CH, dim), BF16), col, col, col, vm((CH, LN), F32),
            row, row, row, vm((SR, LN), jnp.int32),
            stat(2), stat(), stat(NA), stat(), stat(NA), stat(NZ), vm((2, HR + 8, LN), F32),
            vm((2, 2, NA, PZ, dim), F32), vm((NZ, NA, PZ, dim), F32), vm((4, NA, PZ, dim), F32), vm((NZ, NA, PZ, dim), F32),
            vm((4, NA, TD, dim), F32), vm((NZ, NA, TD, dim), F32), vm((2 * NZ, TD, dim), F32),
            DMA((6,)), DMA((5,)), DMA((2,)), DMA((1,))] + Gather.SEMS * 4 + [
            DMA, DMA, DMA((NA,)), DMA((NA,)), DMA, DMA, DMA((NA,)), DMA((NA,)), DMA((NZ - 1,)), DMA((NZ - 1,)), DMA, DMA,
            DMA((NZ,)), DMA((NZ,)), DMA((NZ, NA)), DMA((NZ, NA)), DMA((NZ, NA)), DMA((NZ, NA)), DMA((NZ,)), DMA((NZ,)),
            DMA((3,)), DMA((3,))],
        compiler_params=pltpu.CompilerParams(collective_id=0, has_side_effects=True, vmem_limit_bytes=67043328),
    )(features, w_in, w_out, table, cand_ids.reshape(-1, LN), log_q.reshape(-1, LN), targets)


def fix_kernel(de_ref, h_ref, yl_ref, l_ref, z_ref, out_ref, lst_i, lst_g, si, sg, sem):
    rows = out_ref.shape[0]
    out_ref[...] = de_ref[...]
    yl = yl_ref[...]
    own = (yl >= 0) & (yl < rows)
    g = jnp.where(own, (jnp.exp(jnp.where(own, z_ref[...], 0.0) - l_ref[...]) - 1.0) * (1.0 / NT), 0.0)
    of = jnp.where(own, 1.0, 0.0)
    before = lambda n, i, j: jnp.where(lax.broadcasted_iota(jnp.int32, (n, n), i) < lax.broadcasted_iota(jnp.int32, (n, n), j), 1.0, 0.0).astype(BF16)
    pre = jnp.dot(of.astype(BF16), before(LN, 0, 1), preferred_element_type=F32)
    tot = jnp.broadcast_to(jnp.sum(of, axis=1, keepdims=True), (SR, LN))
    rank = jnp.where(own, pre + jnp.dot(before(SR, 1, 0), tot.astype(BF16), preferred_element_type=F32), -1.0)
    n = jnp.sum(of).astype(jnp.int32)
    lane = lax.broadcasted_iota(jnp.int32, (1, LN), 1)

    def page(p, _):
        slot = (lax.broadcasted_iota(jnp.int32, (LN, LN), 0) + p * LN).astype(F32)
        rr, tt, gg = (jnp.zeros((LN, LN), F32) for _ in range(3))
        for r in range(SR):
            rw = slice(r, r + 1)
            hit = rank[rw] == slot
            rr += jnp.where(hit, yl[rw].astype(F32), 0.0)
            tt += jnp.where(hit, (lane + r * LN).astype(F32), 0.0)
            gg += jnp.where(hit, g[rw], 0.0)
        row = lambda m: jnp.transpose(jnp.broadcast_to(jnp.sum(m, axis=1, keepdims=True), (LN, LN)))[:8]
        lst_i[0] = row(rr).astype(jnp.int32)
        lst_i[1] = row(tt).astype(jnp.int32)
        lst_g[...] = row(gg)
        run([pltpu.make_async_copy(lst_i, si, sem.at[0]), pltpu.make_async_copy(lst_g, sg, sem.at[1])])

        def one(i, _):
            r, t, gv = si[0, 0, i], si[1, 0, i], sg[0, i]
            blk, w = t // TD, t % TD
            ht = h_ref[blk // (NA * NZ * NA), (blk // (NZ * NA)) % NA, (blk // NA) % NZ, blk % NA].astype(F32)
            hr = jnp.sum(jnp.where(lax.broadcasted_iota(jnp.int32, (TD, 1), 0) == w, ht, 0.0), axis=0, keepdims=True)
            out_ref[pl.ds(r, 1), :] += gv * hr
            return 0
        lax.fori_loop(0, jnp.minimum(n - p * LN, LN), one, 0)
        return 0
    lax.fori_loop(0, (n + LN - 1) // LN, page, 0)


def fix(de, h, yl, lr, zr):
    V = pl.BlockSpec(memory_space=pltpu.VMEM)
    return pl.pallas_call(
        fix_kernel, name="fix", out_shape=jax.ShapeDtypeStruct(de.shape, F32), in_specs=[V] * 5, out_specs=V,
        scratch_shapes=[pltpu.VMEM((2, 8, LN), jnp.int32), pltpu.VMEM((8, LN), F32), pltpu.SMEM((2, 8, LN), jnp.int32),
                        pltpu.SMEM((8, LN), F32), DMA((2,))],
        compiler_params=pltpu.CompilerParams(vmem_limit_bytes=20 << 20),
    )(de, h, yl, lr, zr)


def solution(mesh):
    def local_step(*args):
        loss, de, gwi, gwo, h, yl, lr, zr, _ = step(*args)
        return loss.reshape(()), fix(de, h, yl, lr, zr), gwi, gwo

    return jax.shard_map(local_step, mesh=mesh, in_specs=(P("dp", None), P(), P(), P("dp", None), P(), P(), P("dp")), out_specs=(P(), P("dp", None), P(), P()), check_vma=False)
```

time: 1980 us -> 163 us (0.08)
  waiting for transfers between devices: 1490 us -> 0 us
  blocking collectives: 304 us -> 0 us
  Pallas kernels: 0 us -> 148 us
  other arithmetic: 82.3 us -> 0 us
  matrix products: 37.6 us -> 0 us
  local copies, waits for them, and re-layouts: 40.8 us -> 11.2 us
    reduce_scatter x1 -> x0, waiting for transfers between devices: 1280 us -> none  [local_step(): lax.psum_scatter(dq_part, 'dp', scatter_dimension=0, tiled=True)]
    psum x1 -> x0, waiting for transfers between devices: 216 us -> none  [local_step(): lax.psum(jnp.einsum('ti,tf->if', features, d_pre, preferred_element_type=...]
    psum x2 -> x0, blocking collectives: 150 us -> none  [the longest x1 76 us: local_step(): tgt_logit = lax.psum(jnp.where(tgt_own, tgt_dot, 0.0), 'dp')]
    pallas_call x0 -> x2, Pallas kernels: none -> 148 us  [the longest x1 144 us: step(): pl.pallas_call(step_kernel, name='step', out_shape=(sds((1, 1), F32), sds...]
    unnamed x1 -> x0, blocking collectives: 81.9 us -> none
    pmax x1 -> x0, blocking collectives: 72.7 us -> none  [local_step(): lax.pmax(jnp.max(cand_logit, axis=1), 'dp')]
    scatter-add x2 -> x0, other arithmetic: 46.7 us -> none  [local_step(): jnp.zeros(table_blk.shape, jnp.float32).at[cand_index].add(grad_cand)]
    dot_general x7 -> x0, matrix products: 37.6 us -> none  [the longest x1 12.6 us: local_step(): jnp.einsum('td,cd->tc', query_all, cand_rows, preferred_element_type=jnp....]
  transfers between devices with their start and end apart: 3 -> 0, of which waited for: 2 -> 0; matrix products, arithmetic and copies ran while one was open for 4% -> 0% of each run, Pallas kernels for 0% -> 0%
where the time goes in v2:
time: 163 us; the launch traced here: 162 us
  Pallas kernels  148 us (91%)
  local copies, waits for them, and re-layouts  11.2 us (7%)
  between operations  2.42 us (1%)
    pallas_call x1, Pallas kernels, step(): pl.pallas_call(step_kernel, name='step', out_shape=(sds((1, 1), F32), sds...  144 us
    unnamed x14, local copies, waits for them, and re-layouts  11.2 us
    pallas_call x1, Pallas kernels, fix(): pl.pallas_call(fix_kernel, name='fix', out_shape=jax.ShapeDtypeStruct(de....  4.35 us

profile of v2, /device:TPU:1, one launch (start us, length us, event | category | flops | bytes accessed | tf_op | source)
XLA Modules:
  0.0 161.9 jit_solution(17501490974654961325)
XLA Ops:
  0.6 143.9 %step.1 = (f32[1,1]{1,0:T(1,128)}, f32[2048,256]{1,0:T(8,128)}, f32[1024,1024]{1,0:T(8,128)}, f32[1024,256]{1,0:T(8,128)}, bf16[2,4,8,4,16,256]{5,4,3,2,1,0:T(8,...) custom-call(bf16[16,1024]{1,0:T(8,128)(2,1)} %x_hbm.1, ...), custom_call_target="tpu_custom_call" | custom-call | tf_op jit(solution)/shard_map/step/pallas_call | solution.py:485
  144.6 0.0 copy-start
  144.6 1.6 copy-done
  146.2 0.0 copy-start.1
  146.2 1.6 copy-done.1
  147.7 0.0 copy-start.2
  147.7 0.7 copy-done.2
  148.5 0.0 copy-start.3
  148.5 0.7 copy-done.3
  149.2 0.0 copy-start.4
  149.2 0.7 copy-done.4
  149.9 4.4 %fix.1 = f32[2048,256]{1,0:T(8,128)} custom-call(f32[2048,256]{1,0:T(8,128)S(1)} %copy-done, bf16[2,4,8,4,16,256]{5,4,3,2,1,0:T(8,128)(2,1)S(1)} %copy-done.1, s32[32,128]{1,0:T(8,128)S(1)} %copy-done.2, f32[32,128]{1,0:T(8,128)S(1)} %copy-done.3, f32[32,128]{1,0:T(8,128)S(1)} %copy-done.4), custom_call_target="tpu_custom_call" | custom-call | tf_op jit(solution)/shard_map/fix/pallas_call | solution.py:549
  154.9 0.0 copy-start.5
  154.9 4.9 %copy.15 = f32[1024,1024]{1,0:T(8,128)} copy(f32[1024,1024]{1,0:T(8,128)} %get-tuple-element.26) | data formatting | bytes 8388608
  159.8 0.0 copy-done.5
  159.8 1.0 copy.16
Async XLA Ops:
  144.6 1.6 copy-start
  146.2 1.6 copy-start.1
  147.7 0.7 copy-start.2
  148.5 0.7 copy-start.3
  149.2 0.7 copy-start.4
  154.9 4.9 %copy-start.5 = (f32[1024,256]{1,0:T(8,128)S(1)}, f32[1024,256]{1,0:T(8,128)}, u32[]{:S(2)}) copy-start(f32[1024,256]{1,0:T(8,128)} %get-tuple-element.27) | copy-start | bytes 3145732

commit v3 on v2

--- a/solution.py
+++ b/solution.py
@@ -19,6 +19,7 @@
 GR = CH // LN
 F32, BF16 = jnp.float32, jnp.bfloat16
 NEG = -jnp.inf
+VMEM_ALL = 67043328
 MESH = pl.DeviceIdType.MESH
 DMA = pltpu.SemaphoreType.DMA
 
@@ -63,7 +64,7 @@
 
 
 class Gather:
-    SEMS = [DMA((NZ - 1,)), DMA((NZ - 1,)), DMA((NA,)), DMA((NA,)), DMA((NA, NA)), DMA((NA, NA)), DMA((NA,)), DMA((NA,))]
+    SEMS = [DMA] * 5 + [DMA((NA - 1,)), DMA, DMA((NA,))]
 
     def __init__(self, buf, sems, src=None):
         z, y, x, c, v, a = coords()
@@ -73,10 +74,14 @@
         own = buf.at[c, v, z, a]
         col = lambda j: buf.at[c, v, :, (a + NA - j) % NA]
         chunk = lambda j: buf.at[c, (v + NA - j) % NA]
-        self.zc = lambda k: rcopy(own if src is None else src, own, sz.at[k - 1], rz.at[k - 1], to_z(k))
-        self.ac = lambda k: rcopy(col(0), col(0), s2.at[k], r2.at[k], to_2(k))
-        self.vc = lambda k, p: rcopy(col(p), col(p), s1.at[k, p], r1.at[k, p], to_1(k))
-        self.dc = lambda j: rcopy(chunk(j), chunk(j), sd.at[j], rd.at[j], to_c)
+        self.zc = lambda k: rcopy(own if src is None else src, own, sz, rz, to_z(k))
+        self.ac = lambda k: rcopy(col(0), col(0), s2, r2, to_2(k))
+        self.vc = lambda k, p: rcopy(col(p), col(p), s1, r1.at[k - 1], to_1(k))
+        self.dc = lambda j: rcopy(chunk(j), chunk(j), sd, rd.at[j], to_c)
+        self.z_all = rcopy(buf.at[c, v, pl.ds(0, NZ - 1), a], buf.at[c, v, pl.ds(0, NZ - 1), a], sz, rz, to_c)
+        self.a_all = rcopy(buf.at[c, v, :, pl.ds(0, NA - 1)], buf.at[c, v, :, pl.ds(0, NA - 1)], s2, r2, to_c)
+        self.v_one = lambda k: rcopy(chunk(k), chunk(k), s1, r1.at[k - 1], to_c)
+        self.d_all = rcopy(buf.at[c], buf.at[c], sd, rd.at[0], to_c)
 
     def start(self):
         @pl.loop(1, NZ)
@@ -84,35 +89,40 @@
             self.zc(k).start()
 
     def second(self):
-        @pl.loop(1, NZ)
-        def _(k):
-            self.zc(k).wait()
+        self.z_all.wait()
         for k in NEAR:
             self.ac(k).start()
 
     def first(self):
         for k in NEAR:
             self.vc(k, 0).start()
+        self.a_all.wait()
         for j in NEAR:
-            self.ac(j).wait()
             for k in NEAR:
                 self.vc(k, j).start()
         self.dc(0).start()
 
-    def take(self, n):
+    def finish(self):
+        for k in NEAR:
+            self.v_one(k).wait_send()
+        self.d_all.wait_send()
+
+    def place(self, n):
         i, p = n // 2, n % 2
         j = i + (i // 2) * (1 - 2 * (i % 2))
-
-        @pl.when((p == 0) & (i > 0))
-        def _():
-            for q in range(NA):
-                self.vc(j, q).wait()
-            self.dc(j).start()
-
-        @pl.when(p == 1)
-        def _():
-            self.dc(j).wait()
-        return self.c + p * (1 - 2 * self.c), (self.v * (1 - p) + self.a * p + NA - j) % NA
+        return i, p, j, (self.c + p * (1 - 2 * self.c), (self.v * (1 - p) + self.a * p + NA - j) % NA)
+
+    def hand(self, i):
+        j = self.place(2 * i)[2]
+        self.v_one(j).wait_recv()
+        self.dc(j).start()
+
+    def take(self, n, hand=True):
+        i, p, j, cv = self.place(n)
+        if hand:
+            pl.when((p == 0) & (i > 0))(lambda: self.hand(i))
+        pl.when(p == 1)(lambda: self.dc(j).wait_recv())
+        return cv
 
 
 def to_col(row):
@@ -203,12 +213,14 @@
     to_c, to_z, to_1, to_2 = peers()
     sc, rc, s1, r1, ss, rs, s2, r2, sz, rz, sf, rf = sems
 
-    def step(copies, lo=0, hi=0):
+    all3 = lambda b, ss_, rs_: rcopy(b.at[pl.ds(0, NA - 1)], b.at[pl.ds(0, NA - 1)], ss_, rs_, to_c)
+
+    def step(copies, lo=0, hi=0, every=None):
         for cp in copies:
             cp.start()
         if hi:
             fill(lo, hi)
-        for cp in copies:
+        for cp in copies if every is None else [every]:
             cp.wait()
     for hf in range(2):
         hs = slice(hf * HR, (hf + 1) * HR)
@@ -221,13 +233,13 @@
     here, there = b0[c], bc[...]
     even = c == 0
     put_stats(b1.at[a], [jnp.where(even, here, there), jnp.where(even, there, here)])
-    step([rcopy(b1.at[a], b1.at[a], s1.at[k], r1.at[k], to_2(k)) for k in NEAR], 0, 2)
+    step([rcopy(b1.at[a], b1.at[a], s1, r1, to_2(k)) for k in NEAR], 0, 2, all3(b1, s1, r1))
     put_stats(b0.at[c], [b1[i] for i in range(NA)])
     step([rcopy(b0.at[c], bs, ss, rs, to_c)])
     b2[a] = bs[...]
-    step([rcopy(bs, b2.at[a], s2.at[k], r2.at[k], to_2(k)) for k in NEAR], 2, 5)
+    step([rcopy(bs, b2.at[a], s2, r2, to_2(k)) for k in NEAR], 2, 5, all3(b2, s2, r2))
     put_stats(bz.at[z], [b2[i] for i in range(NA)])
-    step([rcopy(bz.at[z], bz.at[z], sz.at[k - 1], rz.at[k - 1], to_z(k)) for k in range(1, NZ)], 5, NC)
+    step([rcopy(bz.at[z], bz.at[z], sz, rz, to_z(k)) for k in range(1, NZ)], 5, NC, rcopy(bz.at[pl.ds(0, NZ - 1)], bz.at[pl.ds(0, NZ - 1)], sz, rz, to_c))
     m, s, t = merge_stats([bz[i] for i in range(NZ)])
     fin[1 - c, :HR, :] = m + jnp.log(s)
     fin[1 - c, HR:, :] = t
@@ -248,9 +260,9 @@
 
 
 def step_kernel(x_hbm, win_hbm, wout_hbm, emb_hbm, cid_hbm, lq_hbm, y_s,
-                loss_ref, de_hbm, gwi_hbm, gwo_hbm, h_hbm, yl_out, l_out, z_out, xg,
+                loss_ref, de_hbm, gwi_hbm, gwo_hbm, h_hbm, st_hbm, lh_hbm, li_hbm, lg_hbm, xg,
                 xv, win, wout, emb, cid_v, lq_v, lqr, hb, yb, dh,
-                eb, pb, de, te, dcol, mcol, zcol, scol, mr, sr, zr, yl,
+                eb, pb, de, te, dcol, mcol, zcol, scol, mr, sr, zr, yl, st, lh, li, lg,
                 b0, bc, b1, bs, b2, bz, fin,
                 dq, rc, a0, ra, a1, rb, zb,
                 lsem, osem, fsem, xsem, *sems):
@@ -283,18 +295,16 @@
     gath, gaty, gatx, gatd = Gather(hb, gh), Gather(yb, gy), Gather(xg, gx, xv), Gather(dh, gd)
     gath.start()
     gaty.start()
-    gatx.start()
     for cp in loads[3:]:
         cp.wait()
     logq_rows(cid_v, lq_v, lqr, base)
     de[...] = jnp.zeros_like(de)
     for g in (gath, gaty):
         g.second()
+    xown.wait()
+    gatx.start()
     for g in (gath, gaty):
         g.first()
-    xown.wait()
-    gatx.second()
-
     def score(cc, vv):
         ci = cc * NA + vv
         target_cols(lambda b: yb[cc, vv, b // NA, b % NA], base, yl, ci * GR, dcol.at[ci])
@@ -309,8 +319,10 @@
     @pl.loop(0, NC)
     def _(n):
         gaty.take(n)
-        score(*gath.take(n))
-        pl.when(n == NA - 1)(gatx.first)
+        cv = gath.take(n)
+        score(*cv)
+        pl.when(n == NA - 1)(gatx.second)
+        pl.when(n == NC - 1)(gatx.first)
 
     def target_rows(lo, hi):
         @pl.loop(lo, hi)
@@ -319,7 +331,7 @@
                 pb[:, q:q + LN] = jnp.where(dcol[ci] == float(q), 1.0, 0.0).astype(BF16)
             te[ci] = jnp.dot(pb[...], emb[...], preferred_element_type=F32).astype(BF16)
 
-    lr = l_out
+    lr = st.at[1]
     loss_ref[0, 0] = reduce_stats(mr, sr, zr, lr, b0, bc, b1, bs, b2, bz, fin, sems[:12], target_rows)
     @pl.loop(0, NC)
     def _(ci):
@@ -329,20 +341,22 @@
             mcol[ci, bs_, :] = jnp.exp(mcol[ci, bs_, :] - lc) * (1.0 / NT)
             zc = zcol[ci, bs_, :]
             zcol[ci, bs_, :] = jnp.where(zc > NEG, (jnp.exp(zc - lc) - 1.0) * (1.0 / NT), 0.0)
-    yl_out[...] = yl[...]
-    z_out[...] = zr[...]
+    st[0] = yl[...].astype(F32)
+    st[2] = zr[...]
 
     sc, rcs, sa, ras, sb, rbs, sz, rzs = sems[12:20]
     ring = a0.shape[0]
-    c_copy = lambda k: rcopy(dq.at[k % 2, 1 - c], rc.at[k], sc.at[k], rcs.at[k], to_c)
-    a_copy = lambda k, j: rcopy(a0.at[k % ring, (v + j) % NA], ra.at[k, v], sa.at[k, j], ras.at[k, j], to_1(j))
-    b_copy = lambda k, j: rcopy(a1.at[k % ring, (a + j) % NA], rb.at[k, a], sb.at[k, j], rbs.at[k, j], to_2(j))
+    c_copy = lambda k: rcopy(dq.at[k % 2, 1 - c], rc.at[k], sc.at[k % 2], rcs.at[k], to_c)
+    a_copy = lambda k, j: rcopy(a0.at[k % ring, (v + j) % NA], ra.at[k, v], sa.at[k % ring], ras.at[k], to_1(j))
+    a_all = lambda k: rcopy(ra.at[k, pl.ds(0, NA - 1)], ra.at[k, pl.ds(0, NA - 1)], sa.at[k % ring], ras.at[k], to_c)
+    b_copy = lambda k, j: rcopy(a1.at[k % ring, (a + j) % NA], rb.at[k, a], sb.at[k % ring], rbs.at[k], to_2(j))
+    b_all = lambda k: rcopy(rb.at[k, pl.ds(0, NA - 1)], rb.at[k, pl.ds(0, NA - 1)], sb.at[k % ring], rbs.at[k], to_c)
 
     def off(k):
         s = (k + 1) // 2
         return NA + s - 2 * s * (k % 2)
 
-    z_copy = lambda k: rcopy(zb.at[NZ + k], zb.at[z], sz.at[k], rzs.at[k], to_z(off(k)))
+    z_copy = lambda k: rcopy(zb.at[NZ + k], zb.at[z], sz, rzs, to_z(off(k)))
 
     def compute(k):
         zz = (z + off(k)) % NZ
@@ -370,16 +384,14 @@
             a_copy(k, j).start()
 
     def sum_first(k):
-        for j in NEAR:
-            a_copy(k, j).wait()
+        a_all(k).wait()
         ra[k, v] = a0[k % ring, v]
         a1[k % ring] = ((ra[k, 0] + ra[k, 1]) + (ra[k, 2] + ra[k, 3])).reshape(NA, TD, 2 * LN)
         for j in NEAR:
             b_copy(k, j).start()
 
     def sum_second(k, last=False):
-        for j in NEAR:
-            b_copy(k, j).wait()
+        b_all(k).wait()
         rb[k, a] = a1[k % ring, a]
         val = (rb[k, 0] + rb[k, 1]) + (rb[k, 2] + rb[k, 3])
         if last:
@@ -392,11 +404,12 @@
         compute(k)
         for lag, f in ((1, sum_core), (3, sum_first), (5, sum_second)):
             pl.when(k >= lag)(functools.partial(f, k - lag))
+        pl.when(k >= NZ - NA + 1)(lambda: gatx.hand(k - (NZ - NA)))
         return 0
 
     lax.fori_loop(0, NZ, body, 0)
-    outs = [pltpu.make_async_copy(de, de_hbm, osem.at[0]), pltpu.make_async_copy(hb, h_hbm, osem.at[1])]
-    for cp in outs:
+    outs = [pltpu.make_async_copy(s, d, osem.at[i]) for i, (s, d) in enumerate(((de, de_hbm), (hb, h_hbm), (st, st_hbm), (lh, lh_hbm), (li, li_hbm), (lg, lg_hbm)))]
+    for cp in outs[:3]:
         cp.start()
 
     cols = pl.ds(pl.multiple_of(c * half, half), half)
@@ -408,38 +421,44 @@
         eb[ci, :, :half] = der
         eb[ci, :, half:2 * half] = act.astype(BF16).astype(F32)
 
+    ordinal = lambda n: gatx.place(n)[3][0] * NA + gatx.place(n)[3][1]
+
+    def towers(lo, hi):
+        @pl.loop(lo, hi)
+        def _(n):
+            @pl.when(n + 1 < NC)
+            def _():
+                gatx.take(n + 1, hand=False)
+                xs(ordinal(n + 1), (n + 1) % 2).start()
+            xs(ordinal(n), n % 2).wait()
+            tower(ordinal(n), n % 2)
+
+    xs(ordinal(0), 0).start()
+    towers(0, 1)
     sum_core(7)
     sum_first(5)
     sum_second(3)
+    towers(1, 2)
     sum_first(6)
     sum_second(4)
     sum_second(5)
+    towers(2, 4)
     sum_first(7)
     sum_second(6)
+    towers(4, 6)
     sum_second(7, last=True)
-    for k in range(NZ - 1):
-        z_copy(k).wait()
+    rcopy(zb.at[pl.ds(0, NZ - 1)], zb.at[pl.ds(0, NZ - 1)], sz, rzs, to_c).wait()
     tot = ((zb[0] + zb[1]) + (zb[2] + zb[3])) + ((zb[4] + zb[5]) + (zb[6] + zb[7]))
     dh[c, v, z, a] = tot.astype(BF16)
     gatd.start()
-    pl.loop(0, NC)(lambda n: gatx.take(n) and None)
-    xs(0, 0).start()
-
-    def towers(lo, hi):
-        @pl.loop(lo, hi)
-        def _(ci):
-            @pl.when(ci + 1 < NC)
-            def _():
-                xs(ci + 1, (ci + 1) % 2).start()
-            xs(ci, ci % 2).wait()
-            tower(ci, ci % 2)
-
-    towers(0, 3)
+    towers(6, NC)
+    xs(ordinal(0), 0).start()
     gatd.second()
-    towers(3, 5)
+    rank, gfac, _ = target_ranks(st, rows)
+    target_page(0, st, rank, gfac, lambda r: token_rows(hb, r), lh, li, lg)
+    for cp in outs[3:6]:
+        cp.start()
     gatd.first()
-    towers(5, NC)
-
     acc_i, acc_o = eb.at[pl.ds(0, 2), :, pl.ds(2 * half, half)], eb.at[2, :, pl.ds(2 * half, 2 * LN)]
     acc_i[...] = jnp.zeros(acc_i.shape, F32)
     acc_o[...] = jnp.zeros(acc_o.shape, F32)
@@ -456,17 +475,18 @@
 
     @pl.loop(0, NC)
     def _(n):
-        cc, vv = gatd.take(n)
-        cp = xs(cc * NA + vv, n % 2)
-        cp.start()
-        cp.wait()
-        weights(cc * NA + vv, n % 2)
-
+        gatd.take(n)
+        pl.when(n + 1 < NC)(lambda: xs(ordinal(n + 1), (n + 1) % 2).start())
+        xs(ordinal(n), n % 2).wait()
+        weights(ordinal(n), n % 2)
+
+    for g in (gath, gaty, gatx, gatd):
+        g.finish()
     so, ro = sems[20:22]
     mine = [(acc_i.at[r], gwi_hbm.at[pl.ds(r * half, half), cols]) for r in range(2)] + [(acc_o, gwo_hbm.at[cols])]
     ends = [rcopy(s, d, so.at[i], ro.at[i], to_c) for i, (s, d) in enumerate(mine)]
-    outs += [pltpu.make_async_copy(s, d, osem.at[2 + i]) for i, (s, d) in enumerate(mine)]
-    for cp in ends + outs[2:]:
+    outs += [pltpu.make_async_copy(s, d, osem.at[6 + i]) for i, (s, d) in enumerate(mine)]
+    for cp in ends + outs[6:]:
         cp.start()
     for cp in ends + outs:
         cp.wait()
@@ -475,7 +495,7 @@
 def step(features, w_in, w_out, table, cand_ids, log_q, targets):
     rows, dim = table.shape
     hid = w_in.shape[1]
-    V, A, S = (pl.BlockSpec(memory_space=m) for m in (pltpu.VMEM, pl.ANY, pltpu.SMEM))
+    A, S = (pl.BlockSpec(memory_space=m) for m in (pl.ANY, pltpu.SMEM))
     sds = jax.ShapeDtypeStruct
     vm = pltpu.VMEM
     tokens = (2, NA, NZ, NA, TD)
@@ -485,78 +505,102 @@
     return pl.pallas_call(
         step_kernel, name="step",
         out_shape=(sds((1, 1), F32), sds((rows, dim), F32), sds((w_in.shape[0], hid), F32), sds((hid, dim), F32), sds(tokens + (dim,), BF16),
-                   sds((SR, LN), jnp.int32), sds((SR, LN), F32), sds((SR, LN), F32), sds(tokens + (w_in.shape[0],), BF16)),
-        in_specs=[A] * 6 + [S], out_specs=(S, A, A, A, A, V, V, V, A),
+                   sds((3, SR, LN), F32), sds((LN, dim), F32), sds((8, LN), jnp.int32), sds((8, LN), F32), sds(tokens + (w_in.shape[0],), BF16)),
+        in_specs=[A] * 6 + [S], out_specs=(S,) + (A,) * 9,
         scratch_shapes=[
             vm(features.shape, BF16), vm(w_in.shape, BF16), vm(w_out.shape, BF16), vm(table.shape, BF16), vm((TD, LN), jnp.int32), vm((TD, LN), F32),
             vm((8, rows), F32), vm(tokens + (dim,), BF16), vm((2, NA, NZ, NA, 1, LN), jnp.int32), vm(tokens + (dim,), BF16),
             vm((NC, CH, rows), F32), vm((CH, rows), BF16), vm((rows, dim), F32), vm((NC, CH, dim), BF16), col, col, col, vm((CH, LN), F32),
-            row, row, row, vm((SR, LN), jnp.int32),
+            row, row, row, vm((SR, LN), jnp.int32), vm((3, SR, LN), F32), vm((LN, dim), F32), vm((8, LN), jnp.int32), vm((8, LN), F32),
             stat(2), stat(), stat(NA), stat(), stat(NA), stat(NZ), vm((2, HR + 8, LN), F32),
             vm((2, 2, NA, PZ, dim), F32), vm((NZ, NA, PZ, dim), F32), vm((4, NA, PZ, dim), F32), vm((NZ, NA, PZ, dim), F32),
             vm((4, NA, TD, dim), F32), vm((NZ, NA, TD, dim), F32), vm((2 * NZ, TD, dim), F32),
-            DMA((6,)), DMA((5,)), DMA((2,)), DMA((1,))] + Gather.SEMS * 4 + [
-            DMA, DMA, DMA((NA,)), DMA((NA,)), DMA, DMA, DMA((NA,)), DMA((NA,)), DMA((NZ - 1,)), DMA((NZ - 1,)), DMA, DMA,
-            DMA((NZ,)), DMA((NZ,)), DMA((NZ, NA)), DMA((NZ, NA)), DMA((NZ, NA)), DMA((NZ, NA)), DMA((NZ,)), DMA((NZ,)),
-            DMA((3,)), DMA((3,))],
-        compiler_params=pltpu.CompilerParams(collective_id=0, has_side_effects=True, vmem_limit_bytes=67043328),
+            DMA((6,)), DMA((9,)), DMA((2,)), DMA((1,))] + Gather.SEMS * 4 + [
+            DMA] * 12 + [DMA((2,)), DMA((NZ,)), DMA((4,)), DMA((NZ,)), DMA((4,)), DMA((NZ,)), DMA, DMA, DMA((3,)), DMA((3,))],
+        compiler_params=pltpu.CompilerParams(collective_id=0, has_side_effects=True, vmem_limit_bytes=VMEM_ALL),
     )(features, w_in, w_out, table, cand_ids.reshape(-1, LN), log_q.reshape(-1, LN), targets)
 
 
-def fix_kernel(de_ref, h_ref, yl_ref, l_ref, z_ref, out_ref, lst_i, lst_g, si, sg, sem):
-    rows = out_ref.shape[0]
-    out_ref[...] = de_ref[...]
-    yl = yl_ref[...]
-    own = (yl >= 0) & (yl < rows)
-    g = jnp.where(own, (jnp.exp(jnp.where(own, z_ref[...], 0.0) - l_ref[...]) - 1.0) * (1.0 / NT), 0.0)
+def target_ranks(st, rows):
+    own = (st[0] >= 0) & (st[0] < rows)
+    g = jnp.where(own, (jnp.exp(jnp.where(own, st[2], 0.0) - st[1]) - 1.0) * (1.0 / NT), 0.0)
     of = jnp.where(own, 1.0, 0.0)
     before = lambda n, i, j: jnp.where(lax.broadcasted_iota(jnp.int32, (n, n), i) < lax.broadcasted_iota(jnp.int32, (n, n), j), 1.0, 0.0).astype(BF16)
     pre = jnp.dot(of.astype(BF16), before(LN, 0, 1), preferred_element_type=F32)
     tot = jnp.broadcast_to(jnp.sum(of, axis=1, keepdims=True), (SR, LN))
-    rank = jnp.where(own, pre + jnp.dot(before(SR, 1, 0), tot.astype(BF16), preferred_element_type=F32), -1.0)
-    n = jnp.sum(of).astype(jnp.int32)
-    lane = lax.broadcasted_iota(jnp.int32, (1, LN), 1)
+    return jnp.where(own, pre + jnp.dot(before(SR, 1, 0), tot.astype(BF16), preferred_element_type=F32), -1.0), g, jnp.sum(of)
+
+
+def target_page(p, st, rank, g, h_row, out_h, out_i, out_g):
+    slot = (lax.broadcasted_iota(jnp.int32, (LN, LN), 0) + p * LN).astype(F32)
+    rr, gg = jnp.zeros((LN, LN), F32), jnp.zeros((LN, LN), F32)
+    hh = jnp.zeros((LN, 2 * LN), F32)
+    for r in range(SR):
+        rw = slice(r, r + 1)
+        hit = rank[rw] == slot
+        rr += jnp.where(hit, st[0, rw], 0.0)
+        gg += jnp.where(hit, g[rw], 0.0)
+        hh += jnp.dot(jnp.where(hit, 1.0, 0.0).astype(BF16), h_row(r), preferred_element_type=F32)
+    row = lambda m: jnp.transpose(jnp.broadcast_to(jnp.sum(m, axis=1, keepdims=True), (LN, LN)))[:8]
+    out_i[...] = row(rr).astype(jnp.int32)
+    out_g[...] = row(gg)
+    out_h[...] = hh
+
+
+def token_rows(h, r):
+    ci, g = r // GR, r % GR
+    return h[ci // NA, ci % NA, 2 * g:2 * g + 2].reshape(LN, 2 * LN)
+
+
+def fix_kernel(de_hbm, h_hbm, st_hbm, lh_hbm, li_hbm, lg_hbm, gwi_hbm, gwo_hbm, out_hbm, wi_hbm, wo_hbm,
+               de, h, st, wi, wo, lh, li, lg, si, sg, sem):
+    rows = de.shape[0]
+    pairs = ((st_hbm, st), (li_hbm, si), (lg_hbm, sg), (lh_hbm, lh), (de_hbm, de), (gwi_hbm, wi), (gwo_hbm, wo), (de, out_hbm), (wi, wi_hbm), (wo, wo_hbm))
+    ins = [pltpu.make_async_copy(s, d, sem.at[i]) for i, (s, d) in enumerate(pairs)]
+    outs = ins[7:]
+    for cp in ins[:7]:
+        cp.start()
+    ins[0].wait()
+    own = (st[0] >= 0) & (st[0] < rows)
+    n = jnp.sum(jnp.where(own, 1.0, 0.0)).astype(jnp.int32)
+    for i in (6, 5):
+        ins[i].wait()
+        ins[i + 3].start()
+    for cp in ins[1:5]:
+        cp.wait()
 
     def page(p, _):
-        slot = (lax.broadcasted_iota(jnp.int32, (LN, LN), 0) + p * LN).astype(F32)
-        rr, tt, gg = (jnp.zeros((LN, LN), F32) for _ in range(3))
-        for r in range(SR):
-            rw = slice(r, r + 1)
-            hit = rank[rw] == slot
-            rr += jnp.where(hit, yl[rw].astype(F32), 0.0)
-            tt += jnp.where(hit, (lane + r * LN).astype(F32), 0.0)
-            gg += jnp.where(hit, g[rw], 0.0)
-        row = lambda m: jnp.transpose(jnp.broadcast_to(jnp.sum(m, axis=1, keepdims=True), (LN, LN)))[:8]
-        lst_i[0] = row(rr).astype(jnp.int32)
-        lst_i[1] = row(tt).astype(jnp.int32)
-        lst_g[...] = row(gg)
-        run([pltpu.make_async_copy(lst_i, si, sem.at[0]), pltpu.make_async_copy(lst_g, sg, sem.at[1])])
-
-        def one(i, _):
-            r, t, gv = si[0, 0, i], si[1, 0, i], sg[0, i]
-            blk, w = t // TD, t % TD
-            ht = h_ref[blk // (NA * NZ * NA), (blk // (NZ * NA)) % NA, (blk // NA) % NZ, blk % NA].astype(F32)
-            hr = jnp.sum(jnp.where(lax.broadcasted_iota(jnp.int32, (TD, 1), 0) == w, ht, 0.0), axis=0, keepdims=True)
-            out_ref[pl.ds(r, 1), :] += gv * hr
-            return 0
-        lax.fori_loop(0, jnp.minimum(n - p * LN, LN), one, 0)
+        @pl.when(p > 0)
+        def _():
+            run([pltpu.make_async_copy(h_hbm, h, sem.at[0])])
+            rank, g, _ = target_ranks(st, rows)
+            target_page(p, st, rank, g, lambda r: token_rows(h, r), lh, li, lg)
+            run([pltpu.make_async_copy(li, si, sem.at[1]), pltpu.make_async_copy(lg, sg, sem.at[2])])
+
+        @pl.loop(0, jnp.minimum(n - p * LN, LN))
+        def _(i):
+            de[pl.ds(si[0, i], 1), :] += sg[0, i] * lh[pl.ds(i, 1), :]
         return 0
     lax.fori_loop(0, (n + LN - 1) // LN, page, 0)
-
-
-def fix(de, h, yl, lr, zr):
-    V = pl.BlockSpec(memory_space=pltpu.VMEM)
+    outs[0].start()
+    for cp in outs:
+        cp.wait()
+
+
+def fix(de, h, st, lh, li, lg, gwi, gwo):
+    A = pl.BlockSpec(memory_space=pl.ANY)
+    vm = lambda m: pltpu.VMEM(m.shape, m.dtype)
+    like = lambda m: jax.ShapeDtypeStruct(m.shape, F32)
     return pl.pallas_call(
-        fix_kernel, name="fix", out_shape=jax.ShapeDtypeStruct(de.shape, F32), in_specs=[V] * 5, out_specs=V,
-        scratch_shapes=[pltpu.VMEM((2, 8, LN), jnp.int32), pltpu.VMEM((8, LN), F32), pltpu.SMEM((2, 8, LN), jnp.int32),
-                        pltpu.SMEM((8, LN), F32), DMA((2,))],
-        compiler_params=pltpu.CompilerParams(vmem_limit_bytes=20 << 20),
-    )(de, h, yl, lr, zr)
+        fix_kernel, name="fix", out_shape=(like(de), like(gwi), like(gwo)), in_specs=[A] * 8, out_specs=(A,) * 3,
+        scratch_shapes=[vm(de), vm(h), vm(st), vm(gwi), vm(gwo), vm(lh), vm(li), vm(lg), pltpu.SMEM(li.shape, jnp.int32), pltpu.SMEM(lg.shape, F32), DMA((10,))],
+        compiler_params=pltpu.CompilerParams(vmem_limit_bytes=VMEM_ALL),
+    )(de, h, st, lh, li, lg, gwi, gwo)
 
 
 def solution(mesh):
     def local_step(*args):
-        loss, de, gwi, gwo, h, yl, lr, zr, _ = step(*args)
-        return loss.reshape(()), fix(de, h, yl, lr, zr), gwi, gwo
+        loss, de, gwi, gwo, *rest, _ = step(*args)
+        return loss.reshape(()), *fix(de, *rest, gwi, gwo)
 
     return jax.shard_map(local_step, mesh=mesh, in_specs=(P("dp", None), P(), P(), P("dp", None), P(), P(), P("dp")), out_specs=(P(), P("dp", None), P(), P()), check_vma=False)

time: 163 us -> 137 us (0.84)
  Pallas kernels: 148 us -> 134 us
  local copies, waits for them, and re-layouts: 11.2 us -> 0 us
    pallas_call x1, Pallas kernels: 144 us -> 128 us  [step(): pl.pallas_call(step_kernel, name='step', out_shape=(sds((1, 1), F32), sds...]
    unnamed x14 -> x0, local copies, waits for them, and re-layouts: 11.2 us -> none
    pallas_call x1, Pallas kernels: 4.35 us -> 6.3 us  [fix(): pl.pallas_call(fix_kernel, name='fix', out_shape=(like(de), like(gwi), li...]
where the time goes in v3:
time: 137 us; the launch traced here: 136 us
  Pallas kernels  134 us (98%)
  between operations  2.34 us (2%)
    pallas_call x1, Pallas kernels, step(): pl.pallas_call(step_kernel, name='step', out_shape=(sds((1, 1), F32), sds...  128 us
    pallas_call x1, Pallas kernels, fix(): pl.pallas_call(fix_kernel, name='fix', out_shape=(like(de), like(gwi), li...  6.3 us

profile of v3, /device:TPU:1, one launch (start us, length us, event | category | flops | bytes accessed | tf_op | source)
XLA Modules:
  0.0 136.5 jit_solution(5665611964208233445)
XLA Ops:
  0.6 127.8 %step.1 = (f32[1,1]{1,0:T(1,128)}, f32[2048,256]{1,0:T(8,128)}, f32[1024,1024]{1,0:T(8,128)}, f32[1024,256]{1,0:T(8,128)}, bf16[2,4,8,4,16,256]{5,4,3,2,1,0:T(8,...) custom-call(bf16[16,1024]{1,0:T(8,128)(2,1)} %x_hbm.1, ...), custom_call_target="tpu_custom_call" | custom-call | tf_op jit(solution)/shard_map/step/pallas_call | solution.py:505
  128.5 6.3 %fix.1 = (f32[2048,256]{1,0:T(8,128)}, f32[1024,1024]{1,0:T(8,128)}, f32[1024,256]{1,0:T(8,128)}) custom-call(f32[2048,256]{1,0:T(8,128)} %get-tuple-element.17.de_hbm, bf16[2,4,8,4,16,256]{5,4,3,2,1,0:T(8,128)(2,1)} %get-tuple-element.18.h_hbm, f32[3,32,128]{2,1,0:T(8,128)} %get-tuple-element.19.st_hbm, f32[128,256]{1,0:T(8,128)} %get-tuple-element.20.lh_hbm, ...), custom_call_target="tpu_custom_call" | custom-call | tf_op jit(solution)/shard_map/fix/pallas_call | solution.py:594

commit v4 on v3

v4 whole, which is shorter than its diff:
```python
import functools
import math
import jax
import jax.numpy as jnp
from jax import lax
from jax.experimental import pallas as pl
from jax.experimental.pallas import tpu as pltpu
from jax.sharding import PartitionSpec as P

NZ, NY, NX = 8, 4, 4
NA = 4
LN = 128
TD = 16
NC = 2 * NA
CH = NZ * NA * TD
NT = NC * CH
PZ = NA * TD
SR = NT // LN
GR = CH // LN
F32, BF16 = jnp.float32, jnp.bfloat16
NEG = -jnp.inf
PER_TOKEN = 1.0 / NT
ZO, AO, PO = NZ - 1, NA - 1, SR - 1
DIM = 2 * LN
NC_LAST = NC - 1
VMEM_ALL = 67043328
MESH = pl.DeviceIdType.MESH
ROWS, COLS = (((0,), (0,)), ((), ())), (((1,), (1,)), ((), ()))
DMA = pltpu.SemaphoreType.DMA


def coords():
    me = lax.axis_index("dp")
    z, y, x, c = me // (NY * NX * 2), (me // (NX * 2)) % NY, (me // 2) % NX, me % 2
    return z, y, x, c, x * (1 - c) + y * c, y * (1 - c) + x * c


def dev(z, y, x, c):
    return (((z * NY + y) * NX + x) * 2 + c,)


def peers():
    z, y, x, c, v, a = coords()
    return (dev(z, y, x, 1 - c), lambda k: dev((z + k) % NZ, y, x, c), lambda k: dev(z, (y + k * c) % NY, (x + k * (1 - c)) % NX, c),
            lambda k: dev(z, (y + k * (1 - c)) % NY, (x + k * c) % NX, c))


def in_plane(k):
    z, y, x, c, v, a = coords()
    p = ((y * NX + x) * 2 + c + k) % SR
    return dev(z, p // (NX * 2), (p // 2) % NX, p % 2)


def rcopy(src, dst, ssem, rsem, to):
    return pltpu.make_async_remote_copy(src_ref=src, dst_ref=dst, send_sem=ssem, recv_sem=rsem, device_id=to, device_id_type=MESH)


def run(copies):
    for cp in copies:
        cp.start()
    for cp in copies:
        cp.wait()


def signal_peers():
    bar = pltpu.get_barrier_semaphore()
    to_c, to_z, to_1, to_2 = peers()
    z, y, x, c, v, a = coords()
    tell = lambda p: pl.semaphore_signal(bar, inc=1, device_id=p, device_id_type=MESH)
    pl.loop(1, NZ)(lambda k: tell(to_z(k)))
    pl.loop(1, SR)(lambda k: tell(in_plane(k)))
    return bar, NZ + SR - 2


NEAR = (1, 3, 2)


class Gather:
    SEMS = [DMA, DMA((2,)), DMA, DMA((3,)), DMA, DMA((AO,)), DMA, DMA((NA,))]
    WAVE = (1, 4, 3)

    def __init__(self, buf, sems):
        z, y, x, c, v, a = coords()
        sz, rz, s2, r2, s1, r1, sd, rd = sems
        to_c, to_z, to_1, to_2 = peers()
        self.c, self.v, self.a = c, v, a
        blk = lambda d, j: buf.at[c, v, (z + NZ - d) % NZ, (a + NA - j) % NA]
        chunk = lambda j: buf.at[c, (v + NA - j) % NA]
        self.to_z = lambda k: rcopy(blk(0, 0), blk(0, 0), sz, rz.at[jnp.minimum(k, NZ - k) // 3], to_z(k)).start()
        self.to_2 = lambda w, d: [rcopy(blk(d, 0), blk(d, 0), s2, r2.at[w], to_2(k)).start() for k in NEAR]
        self.to_1 = lambda d, j: [rcopy(blk(d, j), blk(d, j), s1, r1.at[k - 1], to_1(k)).start() for k in NEAR]
        self.to_c = lambda j: rcopy(chunk(j), chunk(j), sd, rd.at[j], to_c)
        every = lambda ref, ss, rs: rcopy(ref, ref, ss, rs, to_c)
        self.z_in = lambda w: every(buf.at[c, v, pl.ds(0, self.WAVE[w]), a], sz, rz.at[w - 1]).wait_recv()
        self.two_in = lambda w: every(buf.at[c, v, pl.ds(0, (1, AO, AO)[w]), pl.ds(0, (AO, NA, AO)[w])], s2, r2.at[w]).wait_recv()
        self.one_in = lambda k: every(chunk(k), s1, r1.at[k - 1]).wait_recv()
        self.sent = [every(buf.at[c, v, pl.ds(0, ZO), a], sz, rz.at[0]), every(buf.at[c, v, :, pl.ds(0, AO)], s2, r2.at[0]),
                     every(buf.at[c, pl.ds(0, AO)], s1, r1.at[0]), every(buf.at[c], sd, rd.at[0])]

    def each(self, w, f):
        if w == 0:
            f(0)
        else:
            pl.loop(0, self.WAVE[w])(lambda i: f((2 * w - 1 + i // 2) * (1 - 2 * (i % 2))) and None)

    def start(self):
        pl.loop(1, NZ)(self.to_z)
        self.to_2(0, 0)
        self.to_1(0, 0)

    def column(self, w):
        self.z_in(w)
        self.each(w, lambda d: self.to_2(w, d) + self.to_1(d, 0))

    def rest(self, w):
        self.two_in(w)
        self.each(w, lambda d: sum((self.to_1(d, j) for j in NEAR), []))

    def finish(self):
        for cp in self.sent:
            cp.wait_send()

    def place(self, n):
        i, p = n // 2, n % 2
        j = i + (i // 2) * (1 - 2 * (i % 2))
        return i, p, j, (self.c + p * (1 - 2 * self.c), (self.v * (1 - p) + self.a * p + NA - j) % NA)

    def take(self, n):
        i, p, j, cv = self.place(n)

        @pl.when((p == 0) & (i > 0))
        def _():
            self.one_in(j)
            self.to_c(j).start()
        pl.when(p == 1)(lambda: self.to_c(j).wait_recv())
        return cv


class GatherFeatures:
    SEMS = [DMA] * 4 + [DMA, DMA((ZO,)), DMA, DMA((ZO,)), DMA, DMA]

    def __init__(self, buf, sems, src):
        z, y, x, c, v, a = coords()
        s2, r2, s1, r1, sr, rr, sl, rl, sd, rd = sems
        to_c, to_z, to_1, to_2 = peers()
        at = lambda d: buf.at[c, (z + 2 * NZ + d) % NZ]
        own = at(0).at[v // 2, v % 2]
        self.own = own.at[a]
        self.two = lambda: [rcopy(src, own.at[a], s2, r2, to_2(k)).start() for k in NEAR]
        self.one = lambda: [rcopy(own, own, s1, r1, to_1(k)).start() for k in NEAR]
        every = lambda ref, ss, rs: rcopy(ref, ref, ss, rs, to_c)
        self.two_all = every(own.at[pl.ds(0, AO)], s2, r2)
        self.one_all = every(buf.at[c, pl.ds(0, AO), 0, 0], s1, r1)
        self.right = lambda s, h: rcopy(at(1 - s).at[h], at(1 - s).at[h], sr, rr.at[2 * s - 2 + (h if s < NA else 0)], to_z(1))
        self.left = lambda s, h: rcopy(at(s - 1).at[h], at(s - 1).at[h], sl, rl.at[2 * s - 2 + (h if s < NA else 0)], to_z(ZO))
        self.share = lambda ref: rcopy(ref, ref, sd, rd, to_c).start()
        self.at = at
        halves = buf.at[c].reshape((2 * NZ,) + buf.shape[3:])
        self.sent = [every(halves.at[pl.ds(0, ZO)], m, rd) for m in (sr, sl)] + [every(buf.at[c], sd, rd)]
        self.shared = every(buf.at[c], sd, rd)

    def plane(self):
        self.two_all.wait()
        self.one()

    def ring(self):
        self.one_all.wait()
        self.share(self.at(0))
        for h in range(2):
            self.right(1, h).start()
            self.left(1, h).start()

    def move(self, s, h):
        self.right(s, h).wait_recv()
        self.left(s, h).wait_recv()
        if s < 3 or h == 0:
            self.right(s + 1, h).start()
        if s < 3 or h == 1:
            self.left(s + 1, h).start()
        self.share(self.at(-s).at[h])
        self.share(self.at(s).at[h])

    def last(self):
        self.right(NA, 0).wait_recv()
        self.left(NA, 1).wait_recv()
        self.share(self.at(NA))

    def finish(self):
        for cp in self.sent:
            cp.wait_send()


def tree(parts):
    while len(parts) > 1:
        parts = [p + q for p, q in zip(parts[::2], parts[1::2])]
    return parts.pop()


def iota(shape, dim):
    return lax.broadcasted_iota(jnp.int32, shape, dim)


def lane_sum(m):
    return jnp.sum(m, axis=1, keepdims=True)


def lane_max(m):
    return jnp.max(m, axis=1, keepdims=True)


def ones_at(hit):
    return jnp.where(hit, 1.0, 0.0)


def to_col(row):
    return jnp.transpose(jnp.broadcast_to(row, (LN, LN)))


def logq_rows(cid_v, lq_v, lqr_ref, base):
    @pl.loop(0, lqr_ref.shape[1] // LN, unroll=4)
    def _(i):
        blk = pl.multiple_of(i * LN, LN)
        rid = iota((LN, LN), 0) + (base + blk)
        acc = jnp.zeros((LN, LN), F32)
        for q in range(cid_v.shape[0]):
            acc += jnp.where(cid_v[q:q + 1, :] == rid, lq_v[q:q + 1, :], 0.0)
        lqr_ref[:, pl.ds(blk, LN)] = jnp.transpose(jnp.broadcast_to(lane_sum(acc), (LN, LN)))[:8]


def target_cols(yblk, base, yl_ref, row, d_ref):
    lane = iota((LN, LN), 1).astype(F32)
    group = iota((1, LN), 1) // TD
    for g in range(GR):
        yr = sum(jnp.where(group == b, yblk(g * 8 + b), 0) for b in range(8)) - base
        yl_ref[pl.ds(row + g, 1), :] = yr
        d_ref[g * LN:(g + 1) * LN, :] = to_col(yr.astype(F32)) - lane


def scores_chunk(h, emb_ref, lqr_ref, e_ref, d_ref, mcol_ref, zcol_ref, scol_ref):
    rows = emb_ref.shape[0]
    RB = PZ
    for j in range(0, rows, DIM):
        s = lax.dot_general(h, emb_ref[j:j + DIM, :], COLS, preferred_element_type=F32)
        for rb in range(0, CH, RB):
            rs = slice(rb, rb + RB)
            m = mcol_ref[rs, :] if j else jnp.full((RB, LN), NEG, F32)
            zc = zcol_ref[rs, :] if j else jnp.full((RB, LN), NEG, F32)
            d = d_ref[rs, :]
            for k in (0, LN):
                raw = s[rs, k:k + LN]
                hit = d == float(j + k)
                zc = jnp.where(hit, raw, zc)
                val = jnp.where(hit, -1e9, raw - lqr_ref[:1, j + k:j + k + LN])
                e_ref[rs, j + k:j + k + LN] = val
                m = jnp.maximum(m, val)
            mcol_ref[rs, :] = m
            zcol_ref[rs, :] = zc
    for rb in range(0, CH, RB):
        rs = slice(rb, rb + RB)
        zc = lane_max(zcol_ref[rs, :])
        m = jnp.maximum(lane_max(mcol_ref[rs, :]), zc)
        zcol_ref[rs, :] = jnp.broadcast_to(zc, (RB, LN))
        mcol_ref[rs, :] = jnp.broadcast_to(m, (RB, LN))

    def grp(g, _):
        rs = pl.ds(pl.multiple_of(g * RB, RB), RB)
        m = mcol_ref[rs, :]
        tot = jnp.zeros((RB, LN), F32)
        for k in range(0, rows, LN):
            ex = jnp.exp(e_ref[rs, k:k + LN] - m)
            e_ref[rs, k:k + LN] = ex
            tot += ex
        scol_ref[rs, :] = tot
        return 0
    lax.fori_loop(0, CH // RB, grp, 0)
    for rb in range(0, CH, RB):
        rs = slice(rb, rb + RB)
        tot = lane_sum(scol_ref[rs, :])
        scol_ref[rs, :] = jnp.broadcast_to(tot, (RB, LN)) + jnp.exp(zcol_ref[rs, :] - mcol_ref[rs, :])


def reduce_stats(pb, rb, zb, ab, st, sems, fill):
    z, y, x, c, v, a = coords()
    to_c, to_z, to_1, to_2 = peers()
    sp, rp, sz, rz, sa, ra = sems
    me = (y * NX + x) * 2 + c

    def merge(ref):
        m, s = ref[:, 0, :], ref[:, 1, :]
        top = jnp.max(m, axis=0, keepdims=True)
        return top, jnp.sum(s * jnp.exp(m - top), axis=0, keepdims=True), jnp.max(ref[:, 2, :], axis=0, keepdims=True)

    rb[me] = pb[me]
    pl.loop(1, SR)(lambda k: rcopy(pb.at[(me + k) % SR], rb.at[me], sp, rp, in_plane(k)).start())
    fill(0)
    rcopy(rb.at[pl.ds(0, PO)], rb.at[pl.ds(0, PO)], sp, rp, to_c).wait()
    for i, val in enumerate(merge(rb)):
        zb[z, i:i + 1, :] = val
    pl.loop(1, NZ)(lambda k: rcopy(zb.at[z], zb.at[z], sz, rz, to_z(k)).start())
    fill(1)
    rcopy(zb.at[pl.ds(0, ZO)], zb.at[pl.ds(0, ZO)], sz, rz, to_c).wait()
    m, s, t = merge(zb)
    ab[me, 0:1, :] = m + jnp.log(s)
    ab[me, 1:2, :] = t
    pl.loop(1, SR)(lambda k: rcopy(ab.at[me], ab.at[me], sa, ra, in_plane(k)).start())
    fill(2)
    rcopy(ab.at[pl.ds(0, PO)], ab.at[pl.ds(0, PO)], sa, ra, to_c).wait()
    st[1] = ab[:, 0, :]
    st[2] = ab[:, 1, :]
    return jnp.sum(ab[:, 0, :] - ab[:, 1, :]) * PER_TOKEN


def gelu_both(u):
    k0, k1 = math.sqrt(2.0 / math.pi), 0.044715
    sq = u * u
    t = jnp.tanh(k0 * (u + k1 * (sq * u)))
    cdf = 0.5 * (1.0 + t)
    return u * cdf, cdf + (0.5 * k0) * u * ((1.0 - t * t) * (1.0 + (3.0 * k1) * sq))


def step_kernel(x_hbm, win_hbm, wout_hbm, emb_hbm, cid_hbm, lq_hbm, y_s,
                loss_ref, de_hbm, gwi_hbm, gwo_hbm, h_hbm, st_hbm, lh_hbm, li_hbm, lg_hbm, xg,
                xv, win, wout, emb, cid_v, lq_v, lqr, hb, yb, dh,
                eb, pb, de, te, dcol, mcol, zcol, scol, yl, st, lh, li, lg, pst, rst, zst, ast,
                dq, rc, a0, ra, a1, rb, zb,
                lsem, osem, fsem, xsem, *sems):
    z, y, x, c, v, a = coords()
    to_c, to_z, to_1, to_2 = peers()
    rows = emb.shape[0]
    hid = win.shape[1]
    half = hid // 2
    me = lax.axis_index("dp")
    base = me * rows
    take = lambda n, it=iter(sems): [next(it) for _ in range(n)]
    gh, gy, gd = (take(len(Gather.SEMS)) for _ in range(3))
    gx = take(len(GatherFeatures.SEMS))
    own16 = pl.ds(me * TD, TD)
    loads = [pltpu.make_async_copy(s, d, lsem.at[i]) for i, (s, d) in enumerate((
        (x_hbm, xv), (win_hbm, win), (wout_hbm, wout), (emb_hbm, emb), (cid_hbm.at[own16], cid_v), (lq_hbm.at[own16], lq_v)))]
    for cp in loads:
        cp.start()
    bar, n_peers = signal_peers()

    for cp in loads[:3]:
        cp.wait()
    pre = jnp.dot(xv[...], win[...], preferred_element_type=F32)
    act = gelu_both(pre)[0].astype(BF16)
    hb[c, v, z, a] = jnp.dot(act, wout[...], preferred_element_type=F32).astype(BF16)
    lane16 = iota((1, LN), 1) % TD
    yb[c, v, z, a] = sum(jnp.where(lane16 == i, y_s[i], 0) for i in range(TD))
    pl.semaphore_wait(bar, n_peers)

    gath, gaty, gatx, gatd = Gather(hb, gh), Gather(yb, gy), GatherFeatures(xg, gx, xv), Gather(dh, gd)
    xown = pltpu.make_async_copy(xv, gatx.own, xsem.at[0])
    gath.start()
    gaty.start()
    xown.start()
    gatx.two()
    for cp in loads[3:]:
        cp.wait()
    logq_rows(cid_v, lq_v, lqr, base)
    de[...] = jnp.zeros_like(de)
    gath.column(1)
    gaty.column(1)
    gath.rest(0)
    gaty.rest(0)
    xown.wait()
    gatx.plane()
    gath.column(2)
    gaty.column(2)
    gath.rest(1)
    gath.rest(2)
    gath.to_c(0).start()
    gaty.rest(1)
    gaty.rest(2)
    gaty.to_c(0).start()

    lane = iota((LN, LN), 1)

    def score(cc, vv):
        ci = cc * NA + vv
        target_cols(lambda b: yb[cc, vv, b // NA, b % NA], base, yl, ci * GR, dcol.at[ci])
        scores_chunk(hb[cc, vv].reshape(CH, DIM), emb, lqr, eb.at[ci], dcol.at[ci], mcol.at[ci], zcol.at[ci], scol)
        for b in range(GR):
            bs_ = slice(b * LN, (b + 1) * LN)
            three = jnp.where(lane == 0, mcol[ci, bs_, :], jnp.where(lane == 1, scol[bs_, :], zcol[ci, bs_, :]))
            pst[ci * GR + b] = jnp.transpose(three)[:NA]

    @pl.loop(0, NC)
    def _(n):
        gaty.take(n)
        cv = gath.take(n)
        pl.when(n == 1)(gatx.ring)
        pl.when(n == 4)(lambda: gatx.move(1, 0))
        pl.when(n == NC_LAST)(lambda: gatx.move(1, 1))
        score(*cv)

    def target_rows(lo, hi):
        @pl.loop(lo, hi)
        def _(ci):
            for q in range(0, rows, LN):
                pb[:, q:q + LN] = ones_at(dcol[ci] == float(q)).astype(BF16)
            te[ci] = jnp.dot(pb[...], emb[...], preferred_element_type=F32).astype(BF16)

    def fill(n):
        if n:
            gatx.move(2, n - 1)
        target_rows(*((0, 3), (3, 6), (6, NC))[n])

    lr = st.at[1]
    loss_ref[0, 0] = reduce_stats(pst, rst, zst, ast, st, take(6), fill)
    @pl.loop(0, NC)
    def _(ci):
        for b in range(GR):
            bs_ = slice(b * LN, (b + 1) * LN)
            lc = to_col(lr[pl.ds(ci * GR + b, 1), :])
            mcol[ci, bs_, :] = jnp.exp(mcol[ci, bs_, :] - lc) * PER_TOKEN
            zc = zcol[ci, bs_, :]
            zcol[ci, bs_, :] = jnp.where(zc > NEG, (jnp.exp(zc - lc) - 1.0) * PER_TOKEN, 0.0)
    st[0] = yl[...].astype(F32)

    sc, rcs, sa, ras, sb, rbs, sz, rzs = take(8)
    ring = a0.shape[0]
    c_copy = lambda k: rcopy(dq.at[k % 2, 1 - c], rc.at[k], sc.at[k % 2], rcs.at[k], to_c)
    a_copy = lambda k, j: rcopy(a0.at[k % ring, (v + j) % NA], ra.at[k, v], sa.at[k % ring], ras.at[k], to_1(j))
    a_all = lambda k: rcopy(ra.at[k, pl.ds(0, AO)], ra.at[k, pl.ds(0, AO)], sa.at[k % ring], ras.at[k], to_c)
    b_copy = lambda k, j: rcopy(a1.at[k % ring, (a + j) % NA], rb.at[k, a], sb.at[k % ring], rbs.at[k], to_2(j))
    b_all = lambda k: rcopy(rb.at[k, pl.ds(0, AO)], rb.at[k, pl.ds(0, AO)], sb.at[k % ring], rbs.at[k], to_c)

    def off(k):
        s = (k + 1) // 2
        return NA + s - 2 * s * (k % 2)

    z_copy = lambda k: rcopy(zb.at[NZ + k], zb.at[z], sz, rzs, to_z(off(k)))

    def compute(k):
        zz = (z + off(k)) % NZ
        piece = pl.ds(pl.multiple_of(zz * PZ, PZ), PZ)
        for ci in range(NC):
            ps = slice(ci * PZ, (ci + 1) * PZ)
            f = mcol[ci, piece, :]
            for q in range(0, rows, LN):
                pb[ps, q:q + LN] = (eb[ci, piece, q:q + LN] * f).astype(BF16)
        h = jnp.concatenate([hb[ci // NA, ci % NA, zz].reshape(PZ, DIM) for ci in range(NC)], axis=0)
        for q in range(0, rows, CH):
            de[q:q + CH, :] += lax.dot_general(pb[:, q:q + CH], h, ROWS, preferred_element_type=F32)
        out = jnp.dot(pb[...], emb[...], preferred_element_type=F32)
        for ci in range(NC):
            g = zcol[ci, piece, :]
            t = te[ci, piece, :].astype(F32)
            for hf in (0, LN):
                dq[k % 2, ci // NA, ci % NA, :, hf:hf + LN] = out[ci * PZ:(ci + 1) * PZ, hf:hf + LN] + g * t[:, hf:hf + LN]
        c_copy(k).start()

    def sum_core(k):
        c_copy(k).wait()
        a0[k % ring] = dq[k % 2, c] + rc[k]
        for j in NEAR:
            a_copy(k, j).start()

    def sum_first(k):
        a_all(k).wait()
        ra[k, v] = a0[k % ring, v]
        a1[k % ring] = tree([ra[k, i] for i in range(NA)]).reshape(NA, TD, DIM)
        for j in NEAR:
            b_copy(k, j).start()

    def sum_second(k, last=False):
        b_all(k).wait()
        rb[k, a] = a1[k % ring, a]
        val = tree([rb[k, i] for i in range(NA)])
        if last:
            zb[z] = val
        else:
            zb[NZ + k] = val
            z_copy(k).start()

    def body(k, _):
        compute(k)
        for lag, f in ((1, sum_core), (3, sum_first), (5, sum_second)):
            pl.when(k >= lag)(functools.partial(f, k - lag))
        pl.when(k == 1)(lambda: gatx.move(3, 0))
        pl.when(k == 2)(lambda: gatx.move(3, 1))
        pl.when(k == 6)(gatx.last)
        return 0

    lax.fori_loop(0, NZ, body, 0)
    outs = [pltpu.make_async_copy(s, d, osem.at[i]) for i, (s, d) in enumerate(((de, de_hbm), (hb, h_hbm), (st, st_hbm), (lh, lh_hbm), (li, li_hbm), (lg, lg_hbm)))]
    for cp in outs[:3]:
        cp.start()

    cols = pl.ds(pl.multiple_of(c * half, half), half)
    def xs(ci, slot, go):
        to = pl.ds(pl.multiple_of(slot * hid, hid), hid)
        if go:
            @pl.loop(0, NZ)
            def _(zz):
                src = xg.at[ci // NA, zz, (ci % NA) // 2, ci % 2].reshape(PZ, hid)
                pltpu.make_async_copy(src, pb.at[pl.ds(pl.multiple_of(zz * PZ, PZ), PZ), to], fsem.at[slot]).start()
        else:
            pltpu.make_async_copy(pb.at[:, to], pb.at[:, to], fsem.at[slot]).wait()

    def tower(ci, slot):
        pre = jnp.dot(pb[:, pl.ds(pl.multiple_of(slot * hid, hid), hid)], win[:, cols], preferred_element_type=F32)
        act, der = gelu_both(pre)
        eb[ci, :, :half] = der
        eb[ci, :, half:2 * half] = act.astype(BF16).astype(F32)

    ordinal = lambda n: gatd.place(n)[3][0] * NA + gatd.place(n)[3][1]

    def towers(lo, hi):
        @pl.loop(lo, hi)
        def _(n):
            pl.when(n + 1 < NC)(lambda: xs(ordinal(n + 1), (n + 1) % 2, True))
            xs(ordinal(n), n % 2, False)
            tower(ordinal(n), n % 2)

    sum_core(7)
    sum_second(3)
    gatx.shared.wait_recv()
    xs(ordinal(0), 0, True)
    sum_first(5)
    sum_second(4)
    towers(0, 1)
    sum_first(6)
    towers(1, 2)
    sum_first(7)
    sum_second(5)
    towers(2, 3)
    sum_second(6)
    towers(3, 4)
    sum_second(7, last=True)
    rcopy(zb.at[pl.ds(0, ZO)], zb.at[pl.ds(0, ZO)], sz, rzs, to_c).wait()
    tot = tree([zb[i] for i in range(NZ)])
    dh[c, v, z, a] = tot.astype(BF16)
    gatd.start()
    towers(4, 6)
    gatd.column(1)
    gatd.rest(0)
    gatd.column(2)
    towers(6, 7)
    gatd.rest(1)
    towers(7, NC)
    xs(ordinal(0), 0, True)
    gatd.rest(2)
    gatd.to_c(0).start()
    rank, gfac, _ = target_ranks(st, rows)
    target_page(0, st, rank, gfac, lambda r: token_rows(hb, r), lh, li, lg)
    for cp in outs[3:6]:
        cp.start()
    acc_i, acc_o = eb.at[pl.ds(0, 2), :, pl.ds(2 * half, half)], eb.at[2, :, pl.ds(2 * half, DIM)]
    acc_i[...] = jnp.zeros(acc_i.shape, F32)
    acc_o[...] = jnp.zeros(acc_o.shape, F32)

    def weights(ci, slot):
        g = dh[ci // NA, ci % NA].reshape(CH, DIM)
        back = lax.dot_general(g, wout[cols, :], COLS, preferred_element_type=F32)
        da = (eb[ci, :, :half] * back).astype(BF16)
        act = eb[ci, :, half:2 * half].astype(BF16)
        acc_o[...] += lax.dot_general(act, g, ROWS, preferred_element_type=F32)
        for r in range(2):
            xr = pb[:, pl.ds(pl.multiple_of(slot * hid + r * half, half), half)]
            acc_i[r] += lax.dot_general(xr, da, ROWS, preferred_element_type=F32)

    @pl.loop(0, NC)
    def _(n):
        gatd.take(n)
        pl.when(n + 1 < NC)(lambda: xs(ordinal(n + 1), (n + 1) % 2, True))
        xs(ordinal(n), n % 2, False)
        weights(ordinal(n), n % 2)

    for g in (gath, gaty, gatx, gatd):
        g.finish()
    so, ro = take(2)
    mine = [(acc_i.at[r], gwi_hbm.at[pl.ds(r * half, half), cols]) for r in range(2)] + [(acc_o, gwo_hbm.at[cols])]
    ends = [rcopy(s, d, so.at[i], ro.at[i], to_c) for i, (s, d) in enumerate(mine)]
    outs += [pltpu.make_async_copy(s, d, osem.at[6 + i]) for i, (s, d) in enumerate(mine)]
    for cp in ends + outs[6:]:
        cp.start()
    for cp in ends + outs:
        cp.wait()


def step(features, w_in, w_out, table, cand_ids, log_q, targets):
    rows, dim = table.shape
    hid = w_in.shape[1]
    A, S = (pl.BlockSpec(memory_space=m) for m in (pl.ANY, pltpu.SMEM))
    sds = jax.ShapeDtypeStruct
    vm = pltpu.VMEM
    tokens = (2, NA, NZ, NA, TD)
    stat = lambda n: vm((n, NA, LN), F32)
    col = vm((NC, CH, LN), F32)
    return pl.pallas_call(
        step_kernel, name="step",
        out_shape=(sds((1, 1), F32), sds((rows, dim), F32), sds((w_in.shape[0], hid), F32), sds((hid, dim), F32), sds(tokens + (dim,), BF16),
                   sds((3, SR, LN), F32), sds((LN, dim), F32), sds((8, LN), jnp.int32), sds((8, LN), F32), sds((2, NZ, 2, 2, NA, TD, w_in.shape[0]), BF16)),
        in_specs=[A] * 6 + [S], out_specs=(S,) + (A,) * 9,
        scratch_shapes=[
            vm(features.shape, BF16), vm(w_in.shape, BF16), vm(w_out.shape, BF16), vm(table.shape, BF16), vm((TD, LN), jnp.int32), vm((TD, LN), F32),
            vm((8, rows), F32), vm(tokens + (dim,), BF16), vm((2, NA, NZ, NA, 1, LN), jnp.int32), vm(tokens + (dim,), BF16),
            vm((NC, CH, rows), F32), vm((CH, rows), BF16), vm((rows, dim), F32), vm((NC, CH, dim), BF16), col, col, col, vm((CH, LN), F32),
            vm((SR, LN), jnp.int32), vm((3, SR, LN), F32), vm((LN, dim), F32), vm((8, LN), jnp.int32), vm((8, LN), F32),
            stat(SR), stat(SR), stat(NZ), stat(SR),
            vm((2, 2, NA, PZ, dim), F32), vm((NZ, NA, PZ, dim), F32), vm((4, NA, PZ, dim), F32), vm((NZ, NA, PZ, dim), F32),
            vm((4, NA, TD, dim), F32), vm((NZ, NA, TD, dim), F32), vm((2 * NZ, TD, dim), F32),
            DMA((6,)), DMA((9,)), DMA((2,)), DMA((1,))] + Gather.SEMS * 3 + GatherFeatures.SEMS + [
            DMA] * 6 + [DMA((2,)), DMA((NZ,)), DMA((4,)), DMA((NZ,)), DMA((4,)), DMA((NZ,)), DMA, DMA, DMA((3,)), DMA((3,))],
        compiler_params=pltpu.CompilerParams(collective_id=0, has_side_effects=True, vmem_limit_bytes=VMEM_ALL),
    )(features, w_in, w_out, table, cand_ids.reshape(-1, LN), log_q.reshape(-1, LN), targets)


def target_ranks(st, rows):
    own = (st[0] >= 0) & (st[0] < rows)
    g = jnp.where(own, (jnp.exp(jnp.where(own, st[2], 0.0) - st[1]) - 1.0) * PER_TOKEN, 0.0)
    of = ones_at(own)
    before = lambda n, i, j: jnp.where(iota((n, n), i) < iota((n, n), j), 1.0, 0.0).astype(BF16)
    pre = jnp.dot(of.astype(BF16), before(LN, 0, 1), preferred_element_type=F32)
    tot = jnp.broadcast_to(lane_sum(of), (SR, LN))
    return jnp.where(own, pre + jnp.dot(before(SR, 1, 0), tot.astype(BF16), preferred_element_type=F32), -1.0), g, jnp.sum(of)


def target_page(p, st, rank, g, h_row, out_h, out_i, out_g):
    slot = (iota((LN, LN), 0) + p * LN).astype(F32)
    rr, gg = jnp.zeros((LN, LN), F32), jnp.zeros((LN, LN), F32)
    hh = jnp.zeros((LN, DIM), F32)
    for r in range(SR):
        rw = slice(r, r + 1)
        hit = rank[rw] == slot
        rr += jnp.where(hit, st[0, rw], 0.0)
        gg += jnp.where(hit, g[rw], 0.0)
        hh += jnp.dot(ones_at(hit).astype(BF16), h_row(r), preferred_element_type=F32)
    row = lambda m: jnp.transpose(jnp.broadcast_to(lane_sum(m), (LN, LN)))[:8]
    out_i[...] = row(rr).astype(jnp.int32)
    out_g[...] = row(gg)
    out_h[...] = hh


def token_rows(h, r):
    ci, g = r // GR, r % GR
    return h[ci // NA, ci % NA, 2 * g:2 * g + 2].reshape(LN, DIM)


def fix_kernel(de_hbm, h_hbm, st_hbm, lh_hbm, li_hbm, lg_hbm, gwi_hbm, gwo_hbm, out_hbm, wi_hbm, wo_hbm,
               de, h, st, wi, wo, lh, li, lg, si, sg, sem):
    rows = de.shape[0]
    pairs = ((st_hbm, st), (li_hbm, si), (lg_hbm, sg), (lh_hbm, lh), (de_hbm, de), (gwi_hbm, wi), (gwo_hbm, wo), (de, out_hbm), (wi, wi_hbm), (wo, wo_hbm))
    ins = [pltpu.make_async_copy(s, d, sem.at[i]) for i, (s, d) in enumerate(pairs)]
    outs = ins[7:]
    for cp in ins[:7]:
        cp.start()
    ins[0].wait()
    own = (st[0] >= 0) & (st[0] < rows)
    n = jnp.sum(ones_at(own)).astype(jnp.int32)
    for i in (6, 5):
        ins[i].wait()
        ins[i + 3].start()
    for cp in ins[1:5]:
        cp.wait()

    def page(p, _):
        @pl.when(p > 0)
        def _():
            run([pltpu.make_async_copy(h_hbm, h, sem.at[0])])
            rank, g, _ = target_ranks(st, rows)
            target_page(p, st, rank, g, lambda r: token_rows(h, r), lh, li, lg)
            run([pltpu.make_async_copy(li, si, sem.at[1]), pltpu.make_async_copy(lg, sg, sem.at[2])])

        @pl.loop(0, jnp.minimum(n - p * LN, LN))
        def _(i):
            de[pl.ds(si[0, i], 1), :] += sg[0, i] * lh[pl.ds(i, 1), :]
        return 0
    lax.fori_loop(0, (n + LN - 1) // LN, page, 0)
    outs[0].start()
    for cp in outs:
        cp.wait()


def fix(de, h, st, lh, li, lg, gwi, gwo):
    A = pl.BlockSpec(memory_space=pl.ANY)
    vm = lambda m: pltpu.VMEM(m.shape, m.dtype)
    like = lambda m: jax.ShapeDtypeStruct(m.shape, F32)
    return pl.pallas_call(
        fix_kernel, name="fix", out_shape=(like(de), like(gwi), like(gwo)), in_specs=[A] * 8, out_specs=(A,) * 3,
        scratch_shapes=[vm(de), vm(h), vm(st), vm(gwi), vm(gwo), vm(lh), vm(li), vm(lg), pltpu.SMEM(li.shape, jnp.int32), pltpu.SMEM(lg.shape, F32), DMA((10,))],
        compiler_params=pltpu.CompilerParams(vmem_limit_bytes=VMEM_ALL),
    )(de, h, st, lh, li, lg, gwi, gwo)


def solution(mesh):
    def local_step(*args):
        loss, de, gwi, gwo, *rest, _ = step(*args)
        return loss.reshape(()), *fix(de, *rest, gwi, gwo)

    return jax.shard_map(local_step, mesh=mesh, in_specs=(P("dp", None), P(), P(), P("dp", None), P(), P(), P("dp")), out_specs=(P(), P("dp", None), P(), P()), check_vma=False)
```

time: 137 us -> 124 us (0.905)
  Pallas kernels: 134 us -> 122 us
    pallas_call x1, Pallas kernels: 128 us -> 115 us  [step(): pl.pallas_call(step_kernel, name='step', out_shape=(sds((1, 1), F32), sds...]
where the time goes in v4:
time: 124 us
  Pallas kernels  122 us (98%)
  between operations  2.34 us (2%)
    pallas_call x1, Pallas kernels, step(): pl.pallas_call(step_kernel, name='step', out_shape=(sds((1, 1), F32), sds...  115 us
    pallas_call x1, Pallas kernels, fix(): pl.pallas_call(fix_kernel, name='fix', out_shape=(like(de), like(gwi), li...  6.3 us

profile of v4, /device:TPU:1, one launch (start us, length us, event | category | flops | bytes accessed | tf_op | source)
XLA Modules:
  0.0 123.9 jit_solution(12765076990562960038)
XLA Ops:
  0.6 115.2 %step.1 = (f32[1,1]{1,0:T(1,128)}, f32[2048,256]{1,0:T(8,128)}, f32[1024,1024]{1,0:T(8,128)}, f32[1024,256]{1,0:T(8,128)}, bf16[2,4,8,4,16,256]{5,4,3,2,1,0:T(8,...) custom-call(bf16[16,1024]{1,0:T(8,128)(2,1)} %x_hbm.1, ...), custom_call_target="tpu_custom_call" | custom-call | tf_op jit(solution)/shard_map/step/pallas_call | solution.py:593
  115.9 6.3 %fix.1 = (f32[2048,256]{1,0:T(8,128)}, f32[1024,1024]{1,0:T(8,128)}, f32[1024,256]{1,0:T(8,128)}) custom-call(f32[2048,256]{1,0:T(8,128)} %get-tuple-element.17.de_hbm, bf16[2,4,8,4,16,256]{5,4,3,2,1,0:T(8,128)(2,1)} %get-tuple-element.18.h_hbm, f32[3,32,128]{2,1,0:T(8,128)} %get-tuple-element.19.st_hbm, f32[128,256]{1,0:T(8,128)} %get-tuple-element.20.lh_hbm, ...), custom_call_target="tpu_custom_call" | custom-call | tf_op jit(solution)/shard_map/fix/pallas_call | solution.py:682

commit v5 on v4

--- a/solution.py
+++ b/solution.py
@@ -41,14 +41,15 @@
 
 def peers():
     z, y, x, c, v, a = coords()
-    return (dev(z, y, x, 1 - c), lambda k: dev((z + k) % NZ, y, x, c), lambda k: dev(z, (y + k * c) % NY, (x + k * (1 - c)) % NX, c),
-            lambda k: dev(z, (y + k * (1 - c)) % NY, (x + k * c) % NX, c))
+    me = lax.axis_index("dp")
+    one = {k: dev(z, (y + k * c) % NY, (x + k * (1 - c)) % NX, c) for k in range(1, NA)}
+    two = {k: dev(z, (y + k * (1 - c)) % NY, (x + k * c) % NX, c) for k in range(1, NA)}
+    return (me + 1 - 2 * c,), lambda k: ((me + k * SR) % (NZ * SR),), one.get, two.get
 
 
 def in_plane(k):
-    z, y, x, c, v, a = coords()
-    p = ((y * NX + x) * 2 + c + k) % SR
-    return dev(z, p // (NX * 2), (p // 2) % NX, p % 2)
+    me = lax.axis_index("dp")
+    return (me // SR * SR + (me + k) % SR,)
 
 
 def rcopy(src, dst, ssem, rsem, to):
@@ -75,7 +76,28 @@
 NEAR = (1, 3, 2)
 
 
-class Gather:
+class Arrivals:
+    def finish(self):
+        for cp in self.sent:
+            cp.wait_send()
+
+    def place(self, n):
+        i, p = n // 2, n % 2
+        j = i + (i // 2) * (1 - 2 * (i % 2))
+        return i, p, j, (self.c + p * (1 - 2 * self.c), (self.v * (1 - p) + self.a * p + NA - j) % NA)
+
+    def take(self, n):
+        i, p, j, cv = self.place(n)
+
+        @pl.when((p == 0) & (i > 0))
+        def _():
+            self.one_in(j)
+            self.to_c(j).start()
+        pl.when(p == 1)(lambda: self.to_c(j).wait_recv())
+        return cv
+
+
+class Gather(Arrivals):
     SEMS = [DMA, DMA((2,)), DMA, DMA((3,)), DMA, DMA((AO,)), DMA, DMA((NA,))]
     WAVE = (1, 4, 3)
 
@@ -88,7 +110,7 @@
         chunk = lambda j: buf.at[c, (v + NA - j) % NA]
         self.to_z = lambda k: rcopy(blk(0, 0), blk(0, 0), sz, rz.at[jnp.minimum(k, NZ - k) // 3], to_z(k)).start()
         self.to_2 = lambda w, d: [rcopy(blk(d, 0), blk(d, 0), s2, r2.at[w], to_2(k)).start() for k in NEAR]
-        self.to_1 = lambda d, j: [rcopy(blk(d, j), blk(d, j), s1, r1.at[k - 1], to_1(k)).start() for k in NEAR]
+        self.to_1 = lambda d, js: [rcopy(blk(d, j), blk(d, j), s1, r1.at[k - 1], to_1(k)).start() for j in js for k in NEAR]
         self.to_c = lambda j: rcopy(chunk(j), chunk(j), sd, rd.at[j], to_c)
         every = lambda ref, ss, rs: rcopy(ref, ref, ss, rs, to_c)
         self.z_in = lambda w: every(buf.at[c, v, pl.ds(0, self.WAVE[w]), a], sz, rz.at[w - 1]).wait_recv()
@@ -106,34 +128,48 @@
     def start(self):
         pl.loop(1, NZ)(self.to_z)
         self.to_2(0, 0)
-        self.to_1(0, 0)
+        self.to_1(0, (0,))
 
     def column(self, w):
         self.z_in(w)
-        self.each(w, lambda d: self.to_2(w, d) + self.to_1(d, 0))
+        self.each(w, lambda d: self.to_2(w, d) + self.to_1(d, (0,)))
 
     def rest(self, w):
         self.two_in(w)
-        self.each(w, lambda d: sum((self.to_1(d, j) for j in NEAR), []))
-
-    def finish(self):
-        for cp in self.sent:
-            cp.wait_send()
-
-    def place(self, n):
-        i, p = n // 2, n % 2
-        j = i + (i // 2) * (1 - 2 * (i % 2))
-        return i, p, j, (self.c + p * (1 - 2 * self.c), (self.v * (1 - p) + self.a * p + NA - j) % NA)
-
-    def take(self, n):
-        i, p, j, cv = self.place(n)
-
-        @pl.when((p == 0) & (i > 0))
-        def _():
-            self.one_in(j)
-            self.to_c(j).start()
-        pl.when(p == 1)(lambda: self.to_c(j).wait_recv())
-        return cv
+        self.each(w, lambda d: self.to_1(d, NEAR))
+
+
+class GatherSmall(Arrivals):
+    SEMS = [DMA] * 5 + [DMA((AO,)), DMA, DMA((NA,))]
+
+    def __init__(self, buf, sems):
+        z, y, x, c, v, a = coords()
+        sz, rz, s2, r2, s1, r1, sd, rd = sems
+        to_c, to_z, to_1, to_2 = peers()
+        self.c, self.v, self.a = c, v, a
+        own, col = buf.at[c, v, z, a], buf.at[c, v, :, a]
+        chunk = lambda j: buf.at[c, (v + NA - j) % NA]
+        every = lambda ref, ss, rs: rcopy(ref, ref, ss, rs, to_c)
+        self.to_z = lambda k: rcopy(own, own, sz, rz, to_z(k)).start()
+        self.to_2 = lambda: [rcopy(col, col, s2, r2, to_2(k)).start() for k in NEAR]
+        self.to_1 = lambda: [rcopy(chunk(0), chunk(0), s1, r1.at[k - 1], to_1(k)).start() for k in NEAR]
+        self.to_c = lambda j: rcopy(chunk(j), chunk(j), sd, rd.at[j], to_c)
+        self.z_in = every(buf.at[c, v, pl.ds(0, ZO), a], sz, rz)
+        self.two_in = every(buf.at[c, v, :, pl.ds(0, AO)], s2, r2)
+        self.one_in = lambda k: every(chunk(k), s1, r1.at[k - 1]).wait_recv()
+        self.sent = [every(buf.at[c, pl.ds(0, AO)], s1, r1.at[0]), every(buf.at[c], sd, rd.at[0])]
+
+    def start(self):
+        pl.loop(1, NZ)(self.to_z)
+
+    def second(self):
+        self.z_in.wait()
+        self.to_2()
+
+    def first(self):
+        self.two_in.wait()
+        self.to_1()
+        self.to_c(0).start()
 
 
 class GatherFeatures:
@@ -321,7 +357,7 @@
 def step_kernel(x_hbm, win_hbm, wout_hbm, emb_hbm, cid_hbm, lq_hbm, y_s,
                 loss_ref, de_hbm, gwi_hbm, gwo_hbm, h_hbm, st_hbm, lh_hbm, li_hbm, lg_hbm, xg,
                 xv, win, wout, emb, cid_v, lq_v, lqr, hb, yb, dh,
-                eb, pb, de, te, dcol, mcol, zcol, scol, yl, st, lh, li, lg, pst, rst, zst, ast,
+                eb, pb, det, te, dcol, mcol, zcol, scol, yl, st, lh, li, lg, pst, rst, zst, ast,
                 dq, rc, a0, ra, a1, rb, zb,
                 lsem, osem, fsem, xsem, *sems):
     z, y, x, c, v, a = coords()
@@ -332,14 +368,16 @@
     me = lax.axis_index("dp")
     base = me * rows
     take = lambda n, it=iter(sems): [next(it) for _ in range(n)]
-    gh, gy, gd = (take(len(Gather.SEMS)) for _ in range(3))
+    gh, gd, gy = (take(len(Gather.SEMS)) for _ in range(3))
     gx = take(len(GatherFeatures.SEMS))
     own16 = pl.ds(me * TD, TD)
     loads = [pltpu.make_async_copy(s, d, lsem.at[i]) for i, (s, d) in enumerate((
         (x_hbm, xv), (win_hbm, win), (wout_hbm, wout), (emb_hbm, emb), (cid_hbm.at[own16], cid_v), (lq_hbm.at[own16], lq_v)))]
-    for cp in loads:
+    for cp in loads[:2]:
         cp.start()
     bar, n_peers = signal_peers()
+    for cp in loads[2:]:
+        cp.start()
 
     for cp in loads[:3]:
         cp.wait()
@@ -350,7 +388,7 @@
     yb[c, v, z, a] = sum(jnp.where(lane16 == i, y_s[i], 0) for i in range(TD))
     pl.semaphore_wait(bar, n_peers)
 
-    gath, gaty, gatx, gatd = Gather(hb, gh), Gather(yb, gy), GatherFeatures(xg, gx, xv), Gather(dh, gd)
+    gath, gaty, gatx, gatd = Gather(hb, gh), GatherSmall(yb, gy), GatherFeatures(xg, gx, xv), Gather(dh, gd)
     xown = pltpu.make_async_copy(xv, gatx.own, xsem.at[0])
     gath.start()
     gaty.start()
@@ -359,21 +397,17 @@
     for cp in loads[3:]:
         cp.wait()
     logq_rows(cid_v, lq_v, lqr, base)
-    de[...] = jnp.zeros_like(de)
+    det[...] = jnp.zeros_like(det)
     gath.column(1)
-    gaty.column(1)
     gath.rest(0)
-    gaty.rest(0)
     xown.wait()
     gatx.plane()
     gath.column(2)
-    gaty.column(2)
+    gaty.second()
     gath.rest(1)
     gath.rest(2)
     gath.to_c(0).start()
-    gaty.rest(1)
-    gaty.rest(2)
-    gaty.to_c(0).start()
+    gaty.first()
 
     lane = iota((LN, LN), 1)
 
@@ -443,7 +477,7 @@
                 pb[ps, q:q + LN] = (eb[ci, piece, q:q + LN] * f).astype(BF16)
         h = jnp.concatenate([hb[ci // NA, ci % NA, zz].reshape(PZ, DIM) for ci in range(NC)], axis=0)
         for q in range(0, rows, CH):
-            de[q:q + CH, :] += lax.dot_general(pb[:, q:q + CH], h, ROWS, preferred_element_type=F32)
+            det[:, q:q + CH] += lax.dot_general(h, pb[:, q:q + CH], ROWS, preferred_element_type=F32)
         out = jnp.dot(pb[...], emb[...], preferred_element_type=F32)
         for ci in range(NC):
             g = zcol[ci, piece, :]
@@ -477,15 +511,19 @@
 
     def body(k, _):
         compute(k)
-        for lag, f in ((1, sum_core), (3, sum_first), (5, sum_second)):
+        for lag, f in ((1, sum_core), (4, sum_first), (6, sum_second)):
             pl.when(k >= lag)(functools.partial(f, k - lag))
-        pl.when(k == 1)(lambda: gatx.move(3, 0))
-        pl.when(k == 2)(lambda: gatx.move(3, 1))
-        pl.when(k == 6)(gatx.last)
+        pl.when(k == 0)(lambda: gatx.move(3, 0))
+        pl.when(k == 1)(lambda: gatx.move(3, 1))
+        pl.when(k == 7)(gatx.last)
         return 0
 
     lax.fori_loop(0, NZ, body, 0)
-    outs = [pltpu.make_async_copy(s, d, osem.at[i]) for i, (s, d) in enumerate(((de, de_hbm), (hb, h_hbm), (st, st_hbm), (lh, lh_hbm), (li, li_hbm), (lg, lg_hbm)))]
+    de = eb.at[pl.ds(4, 4), :, pl.ds(DIM * 4, DIM)]
+    for q in range(0, rows, LN):
+        for w in (0, LN):
+            de[q // CH, q % CH:q % CH + LN, w:w + LN] = jnp.transpose(det[w:w + LN, q:q + LN])
+    outs = [pltpu.make_async_copy(s, d, osem.at[i]) for i, (s, d) in enumerate(((de, de_hbm.reshape(4, CH, DIM)), (hb, h_hbm), (st, st_hbm), (lh, lh_hbm), (li, li_hbm), (lg, lg_hbm)))]
     for cp in outs[:3]:
         cp.start()
 
@@ -493,10 +531,9 @@
     def xs(ci, slot, go):
         to = pl.ds(pl.multiple_of(slot * hid, hid), hid)
         if go:
-            @pl.loop(0, NZ)
-            def _(zz):
+            for zz in range(NZ):
                 src = xg.at[ci // NA, zz, (ci % NA) // 2, ci % 2].reshape(PZ, hid)
-                pltpu.make_async_copy(src, pb.at[pl.ds(pl.multiple_of(zz * PZ, PZ), PZ), to], fsem.at[slot]).start()
+                pltpu.make_async_copy(src, pb.at[pl.ds(zz * PZ, PZ), to], fsem.at[slot]).start()
         else:
             pltpu.make_async_copy(pb.at[:, to], pb.at[:, to], fsem.at[slot]).wait()
 
@@ -515,21 +552,23 @@
             xs(ordinal(n), n % 2, False)
             tower(ordinal(n), n % 2)
 
+    sum_first(4)
     sum_core(7)
+    sum_second(2)
     sum_second(3)
     gatx.shared.wait_recv()
     xs(ordinal(0), 0, True)
     sum_first(5)
-    sum_second(4)
     towers(0, 1)
     sum_first(6)
+    sum_second(4)
     towers(1, 2)
     sum_first(7)
     sum_second(5)
     towers(2, 3)
     sum_second(6)
+    sum_second(7, last=True)
     towers(3, 4)
-    sum_second(7, last=True)
     rcopy(zb.at[pl.ds(0, ZO)], zb.at[pl.ds(0, ZO)], sz, rzs, to_c).wait()
     tot = tree([zb[i] for i in range(NZ)])
     dh[c, v, z, a] = tot.astype(BF16)
@@ -552,7 +591,13 @@
     acc_i[...] = jnp.zeros(acc_i.shape, F32)
     acc_o[...] = jnp.zeros(acc_o.shape, F32)
 
-    def weights(ci, slot):
+    so, ro = take(2)
+    mine = [(acc_o, gwo_hbm.at[cols])] + [(acc_i.at[r], gwi_hbm.at[pl.ds(r * half, half), cols]) for r in range(2)]
+    ends = [rcopy(s, d, so.at[i], ro.at[i], to_c) for i, (s, d) in enumerate(mine)]
+    outs += [pltpu.make_async_copy(s, d, osem.at[6 + i]) for i, (s, d) in enumerate(mine)]
+    early, late = ends[:2] + outs[6:8], ends[2:] + outs[8:]
+
+    def weights(ci, slot, last=False):
         g = dh[ci // NA, ci % NA].reshape(CH, DIM)
         back = lax.dot_general(g, wout[cols, :], COLS, preferred_element_type=F32)
         da = (eb[ci, :, :half] * back).astype(BF16)
@@ -561,21 +606,24 @@
         for r in range(2):
             xr = pb[:, pl.ds(pl.multiple_of(slot * hid + r * half, half), half)]
             acc_i[r] += lax.dot_general(xr, da, ROWS, preferred_element_type=F32)
-
-    @pl.loop(0, NC)
+            if last and r == 0:
+                for cp in early:
+                    cp.start()
+
+    @pl.loop(0, NC_LAST)
     def _(n):
         gatd.take(n)
-        pl.when(n + 1 < NC)(lambda: xs(ordinal(n + 1), (n + 1) % 2, True))
+        xs(ordinal(n + 1), (n + 1) % 2, True)
         xs(ordinal(n), n % 2, False)
         weights(ordinal(n), n % 2)
 
+    gatd.take(NC_LAST)
+    xs(ordinal(NC_LAST), NC_LAST % 2, False)
+    weights(ordinal(NC_LAST), NC_LAST % 2, last=True)
+
     for g in (gath, gaty, gatx, gatd):
         g.finish()
-    so, ro = take(2)
-    mine = [(acc_i.at[r], gwi_hbm.at[pl.ds(r * half, half), cols]) for r in range(2)] + [(acc_o, gwo_hbm.at[cols])]
-    ends = [rcopy(s, d, so.at[i], ro.at[i], to_c) for i, (s, d) in enumerate(mine)]
-    outs += [pltpu.make_async_copy(s, d, osem.at[6 + i]) for i, (s, d) in enumerate(mine)]
-    for cp in ends + outs[6:]:
+    for cp in late:
         cp.start()
     for cp in ends + outs:
         cp.wait()
@@ -598,12 +646,12 @@
         scratch_shapes=[
             vm(features.shape, BF16), vm(w_in.shape, BF16), vm(w_out.shape, BF16), vm(table.shape, BF16), vm((TD, LN), jnp.int32), vm((TD, LN), F32),
             vm((8, rows), F32), vm(tokens + (dim,), BF16), vm((2, NA, NZ, NA, 1, LN), jnp.int32), vm(tokens + (dim,), BF16),
-            vm((NC, CH, rows), F32), vm((CH, rows), BF16), vm((rows, dim), F32), vm((NC, CH, dim), BF16), col, col, col, vm((CH, LN), F32),
+            vm((NC, CH, rows), F32), vm((CH, rows), BF16), vm((dim, rows), F32), vm((NC, CH, dim), BF16), col, col, col, vm((CH, LN), F32),
             vm((SR, LN), jnp.int32), vm((3, SR, LN), F32), vm((LN, dim), F32), vm((8, LN), jnp.int32), vm((8, LN), F32),
             stat(SR), stat(SR), stat(NZ), stat(SR),
             vm((2, 2, NA, PZ, dim), F32), vm((NZ, NA, PZ, dim), F32), vm((4, NA, PZ, dim), F32), vm((NZ, NA, PZ, dim), F32),
             vm((4, NA, TD, dim), F32), vm((NZ, NA, TD, dim), F32), vm((2 * NZ, TD, dim), F32),
-            DMA((6,)), DMA((9,)), DMA((2,)), DMA((1,))] + Gather.SEMS * 3 + GatherFeatures.SEMS + [
+            DMA((6,)), DMA((9,)), DMA((2,)), DMA((1,))] + Gather.SEMS * 2 + GatherSmall.SEMS + GatherFeatures.SEMS + [
             DMA] * 6 + [DMA((2,)), DMA((NZ,)), DMA((4,)), DMA((NZ,)), DMA((4,)), DMA((NZ,)), DMA, DMA, DMA((3,)), DMA((3,))],
         compiler_params=pltpu.CompilerParams(collective_id=0, has_side_effects=True, vmem_limit_bytes=VMEM_ALL),
     )(features, w_in, w_out, table, cand_ids.reshape(-1, LN), log_q.reshape(-1, LN), targets)

time: 124 us -> 122 us (0.984)
  Pallas kernels: 122 us -> 119 us
    pallas_call x1, Pallas kernels: 115 us -> 113 us  [step(): pl.pallas_call(step_kernel, name='step', out_shape=(sds((1, 1), F32), sds...]
where the time goes in v5:
time: 122 us
  Pallas kernels  119 us (98%)
  between operations  2.34 us (2%)
    pallas_call x1, Pallas kernels, step(): pl.pallas_call(step_kernel, name='step', out_shape=(sds((1, 1), F32), sds...  113 us
    pallas_call x1, Pallas kernels, fix(): pl.pallas_call(fix_kernel, name='fix', out_shape=(like(de), like(gwi), li...  6.3 us

profile of v5, /device:TPU:1, one launch (start us, length us, event | category | flops | bytes accessed | tf_op | source)
XLA Modules:
  0.0 121.5 jit_solution(3374268901350397669)
XLA Ops:
  0.6 112.9 %step.1 = (f32[1,1]{1,0:T(1,128)}, f32[2048,256]{1,0:T(8,128)}, f32[1024,1024]{1,0:T(8,128)}, f32[1024,256]{1,0:T(8,128)}, bf16[2,4,8,4,16,256]{5,4,3,2,1,0:T(8,...) custom-call(bf16[16,1024]{1,0:T(8,128)(2,1)} %x_hbm.1, ...), custom_call_target="tpu_custom_call" | custom-call | tf_op jit(solution)/shard_map/step/pallas_call | solution.py:641
  113.5 6.3 %fix.1 = (f32[2048,256]{1,0:T(8,128)}, f32[1024,1024]{1,0:T(8,128)}, f32[1024,256]{1,0:T(8,128)}) custom-call(f32[2048,256]{1,0:T(8,128)} %get-tuple-element.17.de_hbm, bf16[2,4,8,4,16,256]{5,4,3,2,1,0:T(8,128)(2,1)} %get-tuple-element.18.h_hbm, f32[3,32,128]{2,1,0:T(8,128)} %get-tuple-element.19.st_hbm, f32[128,256]{1,0:T(8,128)} %get-tuple-element.20.lh_hbm, ...), custom_call_target="tpu_custom_call" | custom-call | tf_op jit(solution)/shard_map/fix/pallas_call | solution.py:730

commit v6 on v5

--- a/solution.py
+++ b/solution.py
@@ -425,7 +425,7 @@
         gaty.take(n)
         cv = gath.take(n)
         pl.when(n == 1)(gatx.ring)
-        pl.when(n == 4)(lambda: gatx.move(1, 0))
+        pl.when(n == 5)(lambda: gatx.move(1, 0))
         pl.when(n == NC_LAST)(lambda: gatx.move(1, 1))
         score(*cv)
 
@@ -449,8 +449,7 @@
             bs_ = slice(b * LN, (b + 1) * LN)
             lc = to_col(lr[pl.ds(ci * GR + b, 1), :])
             mcol[ci, bs_, :] = jnp.exp(mcol[ci, bs_, :] - lc) * PER_TOKEN
-            zc = zcol[ci, bs_, :]
-            zcol[ci, bs_, :] = jnp.where(zc > NEG, (jnp.exp(zc - lc) - 1.0) * PER_TOKEN, 0.0)
+            dcol[ci, bs_, :] = lc
     st[0] = yl[...].astype(F32)
 
     sc, rcs, sa, ras, sb, rbs, sz, rzs = take(8)
@@ -480,7 +479,8 @@
             det[:, q:q + CH] += lax.dot_general(h, pb[:, q:q + CH], ROWS, preferred_element_type=F32)
         out = jnp.dot(pb[...], emb[...], preferred_element_type=F32)
         for ci in range(NC):
-            g = zcol[ci, piece, :]
+            zc = zcol[ci, piece, :]
+            g = jnp.where(zc > NEG, (jnp.exp(zc - dcol[ci, piece, :]) - 1.0) * PER_TOKEN, 0.0)
             t = te[ci, piece, :].astype(F32)
             for hf in (0, LN):
                 dq[k % 2, ci // NA, ci % NA, :, hf:hf + LN] = out[ci * PZ:(ci + 1) * PZ, hf:hf + LN] + g * t[:, hf:hf + LN]
@@ -514,7 +514,7 @@
         for lag, f in ((1, sum_core), (4, sum_first), (6, sum_second)):
             pl.when(k >= lag)(functools.partial(f, k - lag))
         pl.when(k == 0)(lambda: gatx.move(3, 0))
-        pl.when(k == 1)(lambda: gatx.move(3, 1))
+        pl.when(k == 2)(lambda: gatx.move(3, 1))
         pl.when(k == 7)(gatx.last)
         return 0
 
@@ -691,17 +691,18 @@
 def fix_kernel(de_hbm, h_hbm, st_hbm, lh_hbm, li_hbm, lg_hbm, gwi_hbm, gwo_hbm, out_hbm, wi_hbm, wo_hbm,
                de, h, st, wi, wo, lh, li, lg, si, sg, sem):
     rows = de.shape[0]
-    pairs = ((st_hbm, st), (li_hbm, si), (lg_hbm, sg), (lh_hbm, lh), (de_hbm, de), (gwi_hbm, wi), (gwo_hbm, wo), (de, out_hbm), (wi, wi_hbm), (wo, wo_hbm))
+    part = [pl.ds(q, CH // 2) for q in range(0, wi.shape[0], CH // 2)]
+    pairs = [(st_hbm, st), (li_hbm, si), (lg_hbm, sg), (lh_hbm, lh), (de_hbm, de), (gwo_hbm, wo)] + [(gwi_hbm.at[q], wi.at[q]) for q in part]
     ins = [pltpu.make_async_copy(s, d, sem.at[i]) for i, (s, d) in enumerate(pairs)]
-    outs = ins[7:]
-    for cp in ins[:7]:
+    outs = [pltpu.make_async_copy(s, d, sem.at[len(ins) + i]) for i, (s, d) in enumerate([(de, out_hbm), (wo, wo_hbm)] + [(wi.at[q], wi_hbm.at[q]) for q in part])]
+    for cp in ins:
         cp.start()
     ins[0].wait()
     own = (st[0] >= 0) & (st[0] < rows)
     n = jnp.sum(ones_at(own)).astype(jnp.int32)
-    for i in (6, 5):
-        ins[i].wait()
-        ins[i + 3].start()
+    for i, o in zip(ins[5:], outs[1:]):
+        i.wait()
+        o.start()
     for cp in ins[1:5]:
         cp.wait()
 
@@ -729,7 +730,7 @@
     like = lambda m: jax.ShapeDtypeStruct(m.shape, F32)
     return pl.pallas_call(
         fix_kernel, name="fix", out_shape=(like(de), like(gwi), like(gwo)), in_specs=[A] * 8, out_specs=(A,) * 3,
-        scratch_shapes=[vm(de), vm(h), vm(st), vm(gwi), vm(gwo), vm(lh), vm(li), vm(lg), pltpu.SMEM(li.shape, jnp.int32), pltpu.SMEM(lg.shape, F32), DMA((10,))],
+        scratch_shapes=[vm(de), vm(h), vm(st), vm(gwi), vm(gwo), vm(lh), vm(li), vm(lg), pltpu.SMEM(li.shape, jnp.int32), pltpu.SMEM(lg.shape, F32), DMA((16,))],
         compiler_params=pltpu.CompilerParams(vmem_limit_bytes=VMEM_ALL),
     )(de, h, st, lh, li, lg, gwi, gwo)
 

time: 122 us -> 121 us (level)
  no operation moved by 1% of the time
where the time goes in v6:
time: 121 us
  Pallas kernels  119 us (98%)
  between operations  2.34 us (2%)
    pallas_call x1, Pallas kernels, step(): pl.pallas_call(step_kernel, name='step', out_shape=(sds((1, 1), F32), sds...  113 us
    pallas_call x1, Pallas kernels, fix(): pl.pallas_call(fix_kernel, name='fix', out_shape=(like(de), like(gwi), li...  5.7 us

profile of v6, /device:TPU:1, one launch (start us, length us, event | category | flops | bytes accessed | tf_op | source)
XLA Modules:
  0.0 121.1 jit_solution(7932550430634282575)
XLA Ops:
  0.6 113.1 %step.1 = (f32[1,1]{1,0:T(1,128)}, f32[2048,256]{1,0:T(8,128)}, f32[1024,1024]{1,0:T(8,128)}, f32[1024,256]{1,0:T(8,128)}, bf16[2,4,8,4,16,256]{5,4,3,2,1,0:T(8,...) custom-call(bf16[16,1024]{1,0:T(8,128)(2,1)} %x_hbm.1, ...), custom_call_target="tpu_custom_call" | custom-call | tf_op jit(solution)/shard_map/step/pallas_call | solution.py:641
  113.7 5.7 %fix.1 = (f32[2048,256]{1,0:T(8,128)}, f32[1024,1024]{1,0:T(8,128)}, f32[1024,256]{1,0:T(8,128)}) custom-call(f32[2048,256]{1,0:T(8,128)} %get-tuple-element.17.de_hbm, bf16[2,4,8,4,16,256]{5,4,3,2,1,0:T(8,128)(2,1)} %get-tuple-element.18.h_hbm, f32[3,32,128]{2,1,0:T(8,128)} %get-tuple-element.19.st_hbm, f32[128,256]{1,0:T(8,128)} %get-tuple-element.20.lh_hbm, ...), custom_call_target="tpu_custom_call" | custom-call | tf_op jit(solution)/shard_map/fix/pallas_call | solution.py:731
